TPU v7x, 512 devices: a whole 4x8x8 slice. The times are simulated.
512 devices in a mesh: win: 128 (over z, y, core), tile: 4 (over x).
Axes of the slice: x: 4, y: 8, z: 8, core: 2. Of those that a mesh axis runs over, the one named last changes fastest.
Arguments:
- right_side: float32 [128, 2, 128, 1024], P('win', None, 'tile'), may hold values from -64 to 64
- error_weight: float32 [128, 2, 128, 1024], P('win', None, 'tile'), may hold values from 0.5 to 4
- coeffs: float32 [4, 128, 2, 128, 1024], P(None, 'win', None, 'tile'), may hold values from 0.1 to 0.4
- obs_block: int32 [128, 128], P('win', 'tile'), may hold values from 0 to 511
- obs_pos: int32 [128, 128, 128], P('win', 'tile'), may hold values from 0 to 127
- obs_weight: float32 [128, 128, 128], P('win', 'tile'), may hold values from 0.5 to 4
Outputs:
- solution_field: float32 [128, 2, 128, 1024], P('win', None, 'tile')
- residual: float32 [128, 2, 128, 1024], P('win', None, 'tile')
All inputs are finite; a program needn't handle non-finite values.
Results may differ from a plain program's by a relative error of at most 0.0001.
Values sent between devices are 32-bit elements; how exact they have to be, the bound alone decides.
No kernel may reach another device: no remote copies, remote signals or barrier semaphores. Data moves between devices by JAX's collectives and lax.ppermute only.
A program may use at most 64 MiB of HBM per device.

v0:
```python
import jax
import jax.numpy as jnp
from jax import lax
from jax.sharding import Mesh
from jax.sharding import PartitionSpec as P

ITERS = 3
WIN = ("win_0", "win_1", "win_2")


def extended(block, sides, width):
    for axis, dim in sides:
        count = lax.axis_size(axis)
        forward = [(i, i + 1) for i in range(count - 1)]
        backward = [(target, source) for source, target in forward]
        low = lax.ppermute(
            lax.slice_in_dim(block, block.shape[dim] - width, None, axis=dim), axis, forward
        )
        high = lax.ppermute(lax.slice_in_dim(block, 0, width, axis=dim), axis, backward)
        block = jnp.concatenate([low, block, high], axis=dim)
    return block


def passed_along(x, axis, by):
    devices = lax.axis_size(axis)
    pairs = [(i, i + by) for i in range(devices) if 0 <= i + by < devices]
    return lax.ppermute(x, axis, pairs)


def sent_to_all(x, axis):
    devices = lax.axis_size(axis)
    return lax.all_to_all(jnp.broadcast_to(x[None], (devices, *x.shape)), axis, 0, 0, tiled=True)


def over_copies(x, axis):
    everything = sent_to_all(x, axis)
    return jnp.sum(everything, axis=0)


def by_axis(x, axes):
    far, near = axes
    nearer = over_copies(x, near)
    return over_copies(nearer, far)


def in_one(arrays, axis):
    ravelled, at, gathered = (jnp.concatenate([a.reshape(-1) for a in arrays]), 0, [])
    running = by_axis(ravelled, axis)
    for a in arrays:
        gathered.append(running[at : at + a.size].reshape(a.shape))
        at += a.size
    return tuple(gathered)


def forward(state, coeffs):
    padded = extended(state, (("tile", 2),), 1)
    north_south = padded[:, :, 2:, :] + padded[:, :, :-2, :]
    return (
        coeffs[0] * state
        + coeffs[1] * north_south
        + coeffs[2] * jnp.roll(state, -1, axis=3)
        + coeffs[3] * jnp.roll(state, 1, axis=3)
    )


def backward(state, coeffs):
    spread = extended(coeffs[1] * state, (("tile", 2),), 1)
    north_south = spread[:, :, 2:, :] + spread[:, :, :-2, :]
    return (
        coeffs[0] * state
        + north_south
        + jnp.roll(coeffs[2] * state, 1, axis=3)
        + jnp.roll(coeffs[3] * state, -1, axis=3)
    )


def observe(state, block_hot, cell_hot, obs_weight):
    width = cell_hot.shape[2]
    block_rows = state.reshape(-1, width)
    picked = jnp.dot(
        block_hot, block_rows, precision=lax.Precision.HIGHEST, preferred_element_type=jnp.float32
    )
    observed = jnp.einsum("bjc,bc->bj", cell_hot, picked, precision=lax.Precision.HIGHEST)
    weighted = observed * obs_weight[0]
    returned = jnp.einsum("bjc,bj->bc", cell_hot, weighted, precision=lax.Precision.HIGHEST)
    spread = jnp.dot(
        block_hot.T, returned, precision=lax.Precision.HIGHEST, preferred_element_type=jnp.float32
    )
    return spread.reshape(state.shape)


def on_device(right_side, error_weight, coeffs, obs_block, obs_pos, obs_weight):
    width = obs_pos.shape[2]
    block_total = right_side.size // width
    block_hot = (obs_block[0][:, None] == jnp.arange(block_total, dtype=jnp.int32)[None, :]).astype(
        jnp.float32
    )
    cell_hot = (obs_pos[0][:, :, None] == jnp.arange(width, dtype=jnp.int32)[None, None, :]).astype(
        jnp.float32
    )
    weight_next = passed_along(error_weight, WIN, -1)

    def hessian(state):
        propagated = forward(state, coeffs)
        before = passed_along(propagated, WIN, 1)
        weighted = error_weight * (state - before)
        later = passed_along(state, WIN, -1)
        following = weight_next * (later - propagated)
        return (
            weighted - backward(following, coeffs) + observe(state, block_hot, cell_hot, obs_weight)
        )

    def two_products(vector, image_vec):
        return in_one(
            (jnp.sum(vector * vector), jnp.sum(vector * image_vec)),
            (("win_0", "win_1"), ("win_2", "tile")),
        )

    solution_field = jnp.zeros_like(right_side)
    residual = right_side
    product_vec = hessian(residual)
    norm_now, product = two_products(residual, product_vec)
    step_length = norm_now / product
    direction = residual
    along = product_vec
    for iteration in range(ITERS):
        solution_field = solution_field + step_length * direction
        residual = residual - step_length * along
        if iteration + 1 < ITERS:
            product_vec = hessian(residual)
            norm_next, product = two_products(residual, product_vec)
            beta_ratio = norm_next / norm_now
            step_length = norm_next / (product - beta_ratio * norm_next / step_length)
            direction = residual + beta_ratio * direction
            along = product_vec + beta_ratio * along
            norm_now = norm_next
    return (solution_field, residual)


def solution(mesh):
    split = Mesh(
        mesh.devices.reshape(8, 8, 2, mesh.shape["tile"]), ("win_0", "win_1", "win_2", "tile")
    )
    in_specs = (
        P(WIN, None, "tile", None),
        P(WIN, None, "tile", None),
        P(None, WIN, None, "tile", None),
        P(WIN, "tile"),
        P(WIN, "tile", None),
        P(WIN, "tile", None),
    )
    out_specs = (P(WIN, None, "tile", None), P(WIN, None, "tile", None))
    return jax.shard_map(
        on_device, mesh=split, in_specs=in_specs, out_specs=out_specs, check_vma=False
    )
```

profile of v0, /device:TPU:1, one launch (start us, length us, event | category | flops | bytes accessed | tf_op | source)
XLA Modules:
  0.0 190.0 jit_solution(7076373985294307808)
XLA Ops:
  0.7 8.9 %collective-permute-start.3 = (f32[1,2,32,1024]{3,2,1,0:T(8,128)}, f32[1,2,32,1024]{3,2,1,0:T(8,128)S(1)}, u32[]{:S(2)}, u32[]{:S(2)}) collective-permute-start(f32[1,2,32,1024]{3,2,1,0:T(8,128)} %param.7), channel_id=1, source_target_pairs={{4,0},{8,4},{12,8},{16,12},{20,16},{24,20},{28,24},{32,28},{36,32}... | collective-permute-start | bytes 786440 | tf_op jit(solution)/shard_map/ppermute | solution.py:27
  9.6 1.9 %collective-permute-start.4 = (f32[1,2,32,1024]{3,2,1,0:T(8,128)}, f32[1,2,32,1024]{3,2,1,0:T(8,128)S(1)}, u32[]{:S(2)}, u32[]{:S(2)}) collective-permute-start(f32[1,2,32,1024]{3,2,1,0:T(8,128)} %param.6), channel_id=1, source_target_pairs={{4,0},{8,4},{12,8},{16,12},{20,16},{24,20},{28,24},{32,28},{36,32}... | collective-permute-start | bytes 786440 | tf_op jit(solution)/shard_map/ppermute | solution.py:27
  13.7 4.0 %collective-permute-start.1 = (f32[1,2,1,1024]{3,2,1,0:T(1,128)S(1)}, f32[1,2,1,1024]{3,2,1,0:T(1,128)S(1)}, u32[]{:S(2)}, u32[]{:S(2)}) collective-permute-start(f32[1,2,1,1024]{3,2,1,0:T(1,128)S(1)} %get-tuple-element.47), channel_id=1, source_target_pairs={{0,1},{1,2},{2,3},{4,5},{5,6},{6,7},{8,9},{9,10},{10,11},{12,13},{... | collective-permute-start | bytes 24584 | tf_op jit(solution)/shard_map/ppermute | solution.py:16
  20.2 2.0 %fusion.5 = f32[32,1,128]{2,1,0:T(1,128)S(1)} fusion(f32[32,128,1]{1,2,0:T(1,128)S(1)} %bitcast.136, s32[32,128]{1,0:T(8,128)S(1)} %bitcast.145), kind=kOutput, calls=%fused_computation.6 | convolution fusion | flops 6815744 | bytes 49152 | tf_op jit(solution)/shard_map/bjc,bc->bj/dot_general | solution.py:83
  22.2 1.5 fusion.4
  24.7 4.3 %collective-permute-start.2 = (f32[1,2,32,1024]{3,2,1,0:T(8,128)}, f32[1,2,32,1024]{3,2,1,0:T(8,128)}, u32[]{:S(2)}, u32[]{:S(2)}) collective-permute-start(f32[1,2,32,1024]{3,2,1,0:T(8,128)} %get-tuple-element.19), channel_id=1, source_target_pairs={{0,4},{4,8},{8,12},{12,16},{16,20},{20,24},{24,28},{28,32},{32,36}... | collective-permute-start | bytes 786440 | tf_op jit(solution)/shard_map/ppermute | solution.py:27
  30.4 4.0 %collective-permute-start.6 = (f32[1,2,1,1024]{3,2,1,0:T(1,128)S(1)}, f32[1,2,1,1024]{3,2,1,0:T(1,128)S(1)}, u32[]{:S(2)}, u32[]{:S(2)}) collective-permute-start(f32[1,2,1,1024]{3,2,1,0:T(1,128)S(1)} %get-tuple-element.45), channel_id=1, source_target_pairs={{0,1},{1,2},{2,3},{4,5},{5,6},{6,7},{8,9},{9,10},{10,11},{12,13},{... | collective-permute-start | bytes 24584 | tf_op jit(solution)/shard_map/ppermute | solution.py:16
  35.2 1.8 multiply_reduce_fusion.5
  38.3 8.3 %all_to_all.36 = f32[8,1,2]{2,1,0:T(1,128)S(1)} all-to-all(f32[8,1,2]{2,1,0:T(1,128)S(1)} %broadcast_in_dim.12), channel_id=1, replica_groups=mesh['win_0'=8,'win_1'=8,'win_2'=2,'tile'=4] {'win_2','tile'}, dimensions={0} | all-to-all | bytes 128 | tf_op jit(solution)/shard_map/all_to_all | solution.py:32
  46.7 22.9 %all_to_all.37 = f32[64,1,2]{2,1,0:T(1,128)S(1)} all-to-all(f32[64,1,2]{2,1,0:T(1,128)S(1)} %broadcast_in_dim.13), channel_id=1, replica_groups=mesh['win_0'=8,'win_1'=8,'win_2'=2,'tile'=4] {'win_0','win_1'}, dimensions={0} | all-to-all | bytes 1024 | tf_op jit(solution)/shard_map/all_to_all | solution.py:32
  71.8 4.0 %collective-permute-start.10 = (f32[1,2,32,1024]{3,2,1,0:T(8,128)S(1)}, f32[1,2,32,1024]{3,2,1,0:T(8,128)S(1)}, u32[]{:S(2)}, u32[]{:S(2)}) collective-permute-start(f32[1,2,32,1024]{3,2,1,0:T(8,128)S(1)} %multiply_subtract_fusion.2), channel_id=1, source_target_pairs={{4,0},{8,4},{12,8},{16,12},{20,16},{24,20},{28,24},{32,28},{36,32}... | collective-permute-start | bytes 786440 | tf_op jit(solution)/shard_map/ppermute | solution.py:27
  77.2 4.0 %collective-permute-start.8 = (f32[1,2,1,1024]{3,2,1,0:T(1,128)S(1)}, f32[1,2,1,1024]{3,2,1,0:T(1,128)S(1)}, u32[]{:S(2)}, u32[]{:S(2)}) collective-permute-start(f32[1,2,1,1024]{3,2,1,0:T(1,128)S(1)} %get-tuple-element.39), channel_id=1, source_target_pairs={{0,1},{1,2},{2,3},{4,5},{5,6},{6,7},{8,9},{9,10},{10,11},{12,13},{... | collective-permute-start | bytes 24584 | tf_op jit(solution)/shard_map/ppermute | solution.py:16
  81.5 2.0 %fusion.3 = f32[32,1,128]{2,1,0:T(1,128)S(1)} fusion(f32[32,128,1]{1,2,0:T(1,128)S(1)} %bitcast.139, s32[32,128]{1,0:T(8,128)S(1)} %bitcast.147), kind=kOutput, calls=%fused_computation.4 | convolution fusion | flops 6815744 | bytes 49152 | tf_op jit(solution)/shard_map/bjc,bc->bj/dot_general | solution.py:83
  83.5 1.5 fusion.2
  85.7 1.9 bitcast_multiply_fusion.1
  87.6 2.7 %collective-permute-start.9 = (f32[1,2,32,1024]{3,2,1,0:T(8,128)}, f32[1,2,32,1024]{3,2,1,0:T(8,128)}, u32[]{:S(2)}, u32[]{:S(2)}) collective-permute-start(f32[1,2,32,1024]{3,2,1,0:T(8,128)} %get-tuple-element.15), channel_id=1, source_target_pairs={{0,4},{4,8},{8,12},{12,16},{16,20},{20,24},{24,28},{28,32},{32,36}... | collective-permute-start | bytes 786440 | tf_op jit(solution)/shard_map/ppermute | solution.py:27
  91.6 4.0 %collective-permute-start.12 = (f32[1,2,1,1024]{3,2,1,0:T(1,128)S(1)}, f32[1,2,1,1024]{3,2,1,0:T(1,128)S(1)}, u32[]{:S(2)}, u32[]{:S(2)}) collective-permute-start(f32[1,2,1,1024]{3,2,1,0:T(1,128)S(1)} %get-tuple-element.37), channel_id=1, source_target_pairs={{0,1},{1,2},{2,3},{4,5},{5,6},{6,7},{8,9},{9,10},{10,11},{12,13},{... | collective-permute-start | bytes 24584 | tf_op jit(solution)/shard_map/ppermute | solution.py:16
  96.8 1.7 reshape.320
  98.7 1.8 multiply_reduce_fusion.3
  101.8 7.9 %all_to_all.38 = f32[8,1,2]{2,1,0:T(1,128)S(1)} all-to-all(f32[8,1,2]{2,1,0:T(1,128)S(1)} %broadcast_in_dim.14), channel_id=1, replica_groups=mesh['win_0'=8,'win_1'=8,'win_2'=2,'tile'=4] {'win_2','tile'}, dimensions={0} | all-to-all | bytes 128 | tf_op jit(solution)/shard_map/all_to_all | solution.py:32
  109.8 15.3 %all_to_all.39 = f32[64,1,2]{2,1,0:T(1,128)S(1)} all-to-all(f32[64,1,2]{2,1,0:T(1,128)S(1)} %broadcast_in_dim.15), channel_id=1, replica_groups=mesh['win_0'=8,'win_1'=8,'win_2'=2,'tile'=4] {'win_0','win_1'}, dimensions={0} | all-to-all | bytes 1024 | tf_op jit(solution)/shard_map/all_to_all | solution.py:32
  131.0 4.0 %collective-permute-start.16 = (f32[1,2,32,1024]{3,2,1,0:T(8,128)S(1)}, f32[1,2,32,1024]{3,2,1,0:T(8,128)S(1)}, u32[]{:S(2)}, u32[]{:S(2)}) collective-permute-start(f32[1,2,32,1024]{3,2,1,0:T(8,128)S(1)} %multiply_subtract_fusion.1), channel_id=1, source_target_pairs={{4,0},{8,4},{12,8},{16,12},{20,16},{24,20},{28,24},{32,28},{36,32}... | collective-permute-start | bytes 786440 | tf_op jit(solution)/shard_map/ppermute | solution.py:27
  136.5 4.0 %collective-permute-start.14 = (f32[1,2,1,1024]{3,2,1,0:T(1,128)S(1)}, f32[1,2,1,1024]{3,2,1,0:T(1,128)S(1)}, u32[]{:S(2)}, u32[]{:S(2)}) collective-permute-start(f32[1,2,1,1024]{3,2,1,0:T(1,128)S(1)} %get-tuple-element.31), channel_id=1, source_target_pairs={{0,1},{1,2},{2,3},{4,5},{5,6},{6,7},{8,9},{9,10},{10,11},{12,13},{... | collective-permute-start | bytes 24584 | tf_op jit(solution)/shard_map/ppermute | solution.py:16
  140.7 2.0 %fusion.1 = f32[32,1,128]{2,1,0:T(1,128)S(1)} fusion(f32[32,128,1]{1,2,0:T(1,128)S(1)} %bitcast.142, s32[32,128]{1,0:T(8,128)S(1)} %bitcast.149), kind=kOutput, calls=%fused_computation.2 | convolution fusion | flops 6815744 | bytes 49152 | tf_op jit(solution)/shard_map/bjc,bc->bj/dot_general | solution.py:83
  142.7 1.5 fusion
  144.9 1.9 bitcast_multiply_fusion
  146.9 2.7 %collective-permute-start.15 = (f32[1,2,32,1024]{3,2,1,0:T(8,128)}, f32[1,2,32,1024]{3,2,1,0:T(8,128)}, u32[]{:S(2)}, u32[]{:S(2)}) collective-permute-start(f32[1,2,32,1024]{3,2,1,0:T(8,128)} %get-tuple-element.11), channel_id=1, source_target_pairs={{0,4},{4,8},{8,12},{12,16},{16,20},{20,24},{24,28},{28,32},{32,36}... | collective-permute-start | bytes 786440 | tf_op jit(solution)/shard_map/ppermute | solution.py:27
  150.9 4.0 %collective-permute-start.18 = (f32[1,2,1,1024]{3,2,1,0:T(1,128)S(1)}, f32[1,2,1,1024]{3,2,1,0:T(1,128)S(1)}, u32[]{:S(2)}, u32[]{:S(2)}) collective-permute-start(f32[1,2,1,1024]{3,2,1,0:T(1,128)S(1)} %get-tuple-element.29), channel_id=1, source_target_pairs={{0,1},{1,2},{2,3},{4,5},{5,6},{6,7},{8,9},{9,10},{10,11},{12,13},{... | collective-permute-start | bytes 24584 | tf_op jit(solution)/shard_map/ppermute | solution.py:16
  156.1 1.7 reshape.326
  158.0 2.0 %multiply_reduce_fusion.1 = (f32[]{:T(128)}, f32[]{:T(128)}, f32[1,2,32,1024]{3,2,1,0:T(8,128)S(1)}) fusion(f32[1,2,32,1024]{3,2,1,0:T(8,128)S(1)} %multiply_subtract_fusion.1, f32[1,2,32,1024]{3,2,1,0:T(8,128)} %reshape.326, f32[1,2,32,1]{3,2,1,0:T(8,128)S(1)} %slice.297, f32[1,2,32,1023]{3,2,1,0:T(8,128)S(1)} %slice.296, ...), kind=kLoop, calls=%fused_computation.83 | loop fusion | flops 1114110 | bytes 2637832 | tf_op jit(solution)/shard_map/reduce_sum | solution.py:115
  161.4 7.9 %all_to_all.40 = f32[8,1,2]{2,1,0:T(1,128)S(1)} all-to-all(f32[8,1,2]{2,1,0:T(1,128)S(1)} %broadcast_in_dim.16), channel_id=1, replica_groups=mesh['win_0'=8,'win_1'=8,'win_2'=2,'tile'=4] {'win_2','tile'}, dimensions={0} | all-to-all | bytes 128 | tf_op jit(solution)/shard_map/all_to_all | solution.py:32
  169.3 15.3 %all_to_all.41 = f32[64,1,2]{2,1,0:T(1,128)S(1)} all-to-all(f32[64,1,2]{2,1,0:T(1,128)S(1)} %broadcast_in_dim.17), channel_id=1, replica_groups=mesh['win_0'=8,'win_1'=8,'win_2'=2,'tile'=4] {'win_0','win_1'}, dimensions={0} | all-to-all | bytes 1024 | tf_op jit(solution)/shard_map/all_to_all | solution.py:32
  (106 shorter events, 26.2 us)
Async XLA Ops:
  0.6 19.2 %copy-start.1 = (f32[1,2,32,1024]{3,2,1,0:T(8,128)S(1)}, f32[1,2,32,1024]{3,2,1,0:T(8,128)}, u32[]{:S(2)}) copy-start(f32[1,2,32,1024]{3,2,1,0:T(8,128)} %param.6) | copy-start | bytes 786436
  0.6 19.3 %copy-start.9 = (s32[1,32]{1,0:T(1,128)S(1)}, s32[1,32]{1,0:T(1,128)}, u32[]{:S(2)}) copy-start(s32[1,32]{1,0:T(1,128)} %param.9) | copy-start | bytes 388
  0.7 19.5 %copy-start.10 = (s32[1,32,128]{2,1,0:T(8,128)S(1)}, s32[1,32,128]{2,1,0:T(8,128)}, u32[]{:S(2)}) copy-start(s32[1,32,128]{2,1,0:T(8,128)} %param.10) | copy-start | bytes 49156
  0.7 23.0 %collective-permute-start.3 = (f32[1,2,32,1024]{3,2,1,0:T(8,128)}, f32[1,2,32,1024]{3,2,1,0:T(8,128)S(1)}, u32[]{:S(2)}, u32[]{:S(2)}) collective-permute-start(f32[1,2,32,1024]{3,2,1,0:T(8,128)} %param.7), channel_id=1, source_target_pairs={{4,0},{8,4},{12,8},{16,12},{20,16},{24,20},{28,24},{32,28},{36,32}... | collective-permute-start | bytes 786440 | tf_op jit(solution)/shard_map/ppermute | solution.py:27
  9.6 14.2 %collective-permute-start.4 = (f32[1,2,32,1024]{3,2,1,0:T(8,128)}, f32[1,2,32,1024]{3,2,1,0:T(8,128)S(1)}, u32[]{:S(2)}, u32[]{:S(2)}) collective-permute-start(f32[1,2,32,1024]{3,2,1,0:T(8,128)} %param.6), channel_id=1, source_target_pairs={{4,0},{8,4},{12,8},{16,12},{20,16},{24,20},{28,24},{32,28},{36,32}... | collective-permute-start | bytes 786440 | tf_op jit(solution)/shard_map/ppermute | solution.py:27
  12.4 11.3 %collective-permute-start = (f32[1,2,1,1024]{3,2,1,0:T(1,128)S(1)}, f32[1,2,1,1024]{3,2,1,0:T(1,128)S(1)}, u32[]{:S(2)}, u32[]{:S(2)}) collective-permute-start(f32[1,2,1,1024]{3,2,1,0:T(1,128)S(1)} %get-tuple-element.46), channel_id=1, source_target_pairs={{1,0},{2,1},{3,2},{5,4},{6,5},{7,6},{9,8},{10,9},{11,10},{13,12},{... | collective-permute-start | bytes 24584 | tf_op jit(solution)/shard_map/ppermute | solution.py:19
  13.7 10.0 %collective-permute-start.1 = (f32[1,2,1,1024]{3,2,1,0:T(1,128)S(1)}, f32[1,2,1,1024]{3,2,1,0:T(1,128)S(1)}, u32[]{:S(2)}, u32[]{:S(2)}) collective-permute-start(f32[1,2,1,1024]{3,2,1,0:T(1,128)S(1)} %get-tuple-element.47), channel_id=1, source_target_pairs={{0,1},{1,2},{2,3},{4,5},{5,6},{6,7},{8,9},{9,10},{10,11},{12,13},{... | collective-permute-start | bytes 24584 | tf_op jit(solution)/shard_map/ppermute | solution.py:16
  18.7 3.5 %copy-start.8 = (f32[1,32,128]{2,1,0:T(8,128)S(1)}, f32[1,32,128]{2,1,0:T(8,128)}, u32[]{:S(2)}) copy-start(f32[1,32,128]{2,1,0:T(8,128)} %param.11) | copy-start | bytes 49156
  20.2 3.5 %copy-start = (f32[4,1,2,32,1024]{4,3,2,1,0:T(8,128)S(1)}, f32[4,1,2,32,1024]{4,3,2,1,0:T(8,128)}, u32[]{:S(2)}) copy-start(f32[4,1,2,32,1024]{4,3,2,1,0:T(8,128)} %param.8) | copy-start | bytes 3145732
  24.7 10.5 %copy-start.2 = (f32[1,2,32,1024]{3,2,1,0:T(8,128)S(1)}, f32[1,2,32,1024]{3,2,1,0:T(8,128)}, u32[]{:S(2)}) copy-start(f32[1,2,32,1024]{3,2,1,0:T(8,128)} %param.7) | copy-start | bytes 786436
  24.7 10.5 %collective-permute-start.2 = (f32[1,2,32,1024]{3,2,1,0:T(8,128)}, f32[1,2,32,1024]{3,2,1,0:T(8,128)}, u32[]{:S(2)}, u32[]{:S(2)}) collective-permute-start(f32[1,2,32,1024]{3,2,1,0:T(8,128)} %get-tuple-element.19), channel_id=1, source_target_pairs={{0,4},{4,8},{8,12},{12,16},{16,20},{20,24},{24,28},{28,32},{32,36}... | collective-permute-start | bytes 786440 | tf_op jit(solution)/shard_map/ppermute | solution.py:27
  29.1 6.0 %collective-permute-start.5 = (f32[1,2,1,1024]{3,2,1,0:T(1,128)S(1)}, f32[1,2,1,1024]{3,2,1,0:T(1,128)S(1)}, u32[]{:S(2)}, u32[]{:S(2)}) collective-permute-start(f32[1,2,1,1024]{3,2,1,0:T(1,128)S(1)} %get-tuple-element.44), channel_id=1, source_target_pairs={{1,0},{2,1},{3,2},{5,4},{6,5},{7,6},{9,8},{10,9},{11,10},{13,12},{... | collective-permute-start | bytes 24584 | tf_op jit(solution)/shard_map/ppermute | solution.py:19
  30.4 4.8 %collective-permute-start.6 = (f32[1,2,1,1024]{3,2,1,0:T(1,128)S(1)}, f32[1,2,1,1024]{3,2,1,0:T(1,128)S(1)}, u32[]{:S(2)}, u32[]{:S(2)}) collective-permute-start(f32[1,2,1,1024]{3,2,1,0:T(1,128)S(1)} %get-tuple-element.45), channel_id=1, source_target_pairs={{0,1},{1,2},{2,3},{4,5},{5,6},{6,7},{8,9},{9,10},{10,11},{12,13},{... | collective-permute-start | bytes 24584 | tf_op jit(solution)/shard_map/ppermute | solution.py:16
  71.8 13.2 %collective-permute-start.10 = (f32[1,2,32,1024]{3,2,1,0:T(8,128)S(1)}, f32[1,2,32,1024]{3,2,1,0:T(8,128)S(1)}, u32[]{:S(2)}, u32[]{:S(2)}) collective-permute-start(f32[1,2,32,1024]{3,2,1,0:T(8,128)S(1)} %multiply_subtract_fusion.2), channel_id=1, source_target_pairs={{4,0},{8,4},{12,8},{16,12},{20,16},{24,20},{28,24},{32,28},{36,32}... | collective-permute-start | bytes 786440 | tf_op jit(solution)/shard_map/ppermute | solution.py:27
  75.9 9.0 %collective-permute-start.7 = (f32[1,2,1,1024]{3,2,1,0:T(1,128)S(1)}, f32[1,2,1,1024]{3,2,1,0:T(1,128)S(1)}, u32[]{:S(2)}, u32[]{:S(2)}) collective-permute-start(f32[1,2,1,1024]{3,2,1,0:T(1,128)S(1)} %get-tuple-element.38), channel_id=1, source_target_pairs={{1,0},{2,1},{3,2},{5,4},{6,5},{7,6},{9,8},{10,9},{11,10},{13,12},{... | collective-permute-start | bytes 24584 | tf_op jit(solution)/shard_map/ppermute | solution.py:19
  77.2 7.7 %collective-permute-start.8 = (f32[1,2,1,1024]{3,2,1,0:T(1,128)S(1)}, f32[1,2,1,1024]{3,2,1,0:T(1,128)S(1)}, u32[]{:S(2)}, u32[]{:S(2)}) collective-permute-start(f32[1,2,1,1024]{3,2,1,0:T(1,128)S(1)} %get-tuple-element.39), channel_id=1, source_target_pairs={{0,1},{1,2},{2,3},{4,5},{5,6},{6,7},{8,9},{9,10},{10,11},{12,13},{... | collective-permute-start | bytes 24584 | tf_op jit(solution)/shard_map/ppermute | solution.py:16
  85.0 0.7 copy-start.7
  87.6 11.1 %collective-permute-start.9 = (f32[1,2,32,1024]{3,2,1,0:T(8,128)}, f32[1,2,32,1024]{3,2,1,0:T(8,128)}, u32[]{:S(2)}, u32[]{:S(2)}) collective-permute-start(f32[1,2,32,1024]{3,2,1,0:T(8,128)} %get-tuple-element.15), channel_id=1, source_target_pairs={{0,4},{4,8},{8,12},{12,16},{16,20},{20,24},{24,28},{28,32},{32,36}... | collective-permute-start | bytes 786440 | tf_op jit(solution)/shard_map/ppermute | solution.py:27
  90.3 8.4 %collective-permute-start.11 = (f32[1,2,1,1024]{3,2,1,0:T(1,128)S(1)}, f32[1,2,1,1024]{3,2,1,0:T(1,128)S(1)}, u32[]{:S(2)}, u32[]{:S(2)}) collective-permute-start(f32[1,2,1,1024]{3,2,1,0:T(1,128)S(1)} %get-tuple-element.36), channel_id=1, source_target_pairs={{1,0},{2,1},{3,2},{5,4},{6,5},{7,6},{9,8},{10,9},{11,10},{13,12},{... | collective-permute-start | bytes 24584 | tf_op jit(solution)/shard_map/ppermute | solution.py:19
  91.6 7.1 %collective-permute-start.12 = (f32[1,2,1,1024]{3,2,1,0:T(1,128)S(1)}, f32[1,2,1,1024]{3,2,1,0:T(1,128)S(1)}, u32[]{:S(2)}, u32[]{:S(2)}) collective-permute-start(f32[1,2,1,1024]{3,2,1,0:T(1,128)S(1)} %get-tuple-element.37), channel_id=1, source_target_pairs={{0,1},{1,2},{2,3},{4,5},{5,6},{6,7},{8,9},{9,10},{10,11},{12,13},{... | collective-permute-start | bytes 24584 | tf_op jit(solution)/shard_map/ppermute | solution.py:16
  131.0 13.2 %collective-permute-start.16 = (f32[1,2,32,1024]{3,2,1,0:T(8,128)S(1)}, f32[1,2,32,1024]{3,2,1,0:T(8,128)S(1)}, u32[]{:S(2)}, u32[]{:S(2)}) collective-permute-start(f32[1,2,32,1024]{3,2,1,0:T(8,128)S(1)} %multiply_subtract_fusion.1), channel_id=1, source_target_pairs={{4,0},{8,4},{12,8},{16,12},{20,16},{24,20},{28,24},{32,28},{36,32}... | collective-permute-start | bytes 786440 | tf_op jit(solution)/shard_map/ppermute | solution.py:27
  135.2 9.0 %collective-permute-start.13 = (f32[1,2,1,1024]{3,2,1,0:T(1,128)S(1)}, f32[1,2,1,1024]{3,2,1,0:T(1,128)S(1)}, u32[]{:S(2)}, u32[]{:S(2)}) collective-permute-start(f32[1,2,1,1024]{3,2,1,0:T(1,128)S(1)} %get-tuple-element.30), channel_id=1, source_target_pairs={{1,0},{2,1},{3,2},{5,4},{6,5},{7,6},{9,8},{10,9},{11,10},{13,12},{... | collective-permute-start | bytes 24584 | tf_op jit(solution)/shard_map/ppermute | solution.py:19
  136.5 7.7 %collective-permute-start.14 = (f32[1,2,1,1024]{3,2,1,0:T(1,128)S(1)}, f32[1,2,1,1024]{3,2,1,0:T(1,128)S(1)}, u32[]{:S(2)}, u32[]{:S(2)}) collective-permute-start(f32[1,2,1,1024]{3,2,1,0:T(1,128)S(1)} %get-tuple-element.31), channel_id=1, source_target_pairs={{0,1},{1,2},{2,3},{4,5},{5,6},{6,7},{8,9},{9,10},{10,11},{12,13},{... | collective-permute-start | bytes 24584 | tf_op jit(solution)/shard_map/ppermute | solution.py:16
  140.7 4.2 %copy-start.4 = (f32[1,2,32,1023]{3,2,1,0:T(8,128)S(1)}, f32[1,2,32,1023]{3,2,1,0:T(8,128)}, u32[]{:S(2)}) copy-start(f32[1,2,32,1023]{3,2,1,0:T(8,128)} %get-tuple-element.32) | copy-start | bytes 785668
  140.7 4.2 %copy-start.5 = (f32[1,2,32,1023]{3,2,1,0:T(8,128)S(1)}, f32[1,2,32,1023]{3,2,1,0:T(8,128)}, u32[]{:S(2)}) copy-start(f32[1,2,32,1023]{3,2,1,0:T(8,128)} %get-tuple-element.33) | copy-start | bytes 785668
  144.2 0.7 copy-start.6
  146.9 2.7 %copy-start.3 = (f32[1,2,32,1024]{3,2,1,0:T(8,128)}, f32[1,2,32,1024]{3,2,1,0:T(8,128)S(1)}, u32[]{:S(2)}) copy-start(f32[1,2,32,1024]{3,2,1,0:T(8,128)S(1)} %get-tuple-element.20) | copy-start | bytes 786436
  146.9 11.1 %collective-permute-start.15 = (f32[1,2,32,1024]{3,2,1,0:T(8,128)}, f32[1,2,32,1024]{3,2,1,0:T(8,128)}, u32[]{:S(2)}, u32[]{:S(2)}) collective-permute-start(f32[1,2,32,1024]{3,2,1,0:T(8,128)} %get-tuple-element.11), channel_id=1, source_target_pairs={{0,4},{4,8},{8,12},{12,16},{16,20},{20,24},{24,28},{28,32},{32,36}... | collective-permute-start | bytes 786440 | tf_op jit(solution)/shard_map/ppermute | solution.py:27
  149.6 8.4 %collective-permute-start.17 = (f32[1,2,1,1024]{3,2,1,0:T(1,128)S(1)}, f32[1,2,1,1024]{3,2,1,0:T(1,128)S(1)}, u32[]{:S(2)}, u32[]{:S(2)}) collective-permute-start(f32[1,2,1,1024]{3,2,1,0:T(1,128)S(1)} %get-tuple-element.28), channel_id=1, source_target_pairs={{1,0},{2,1},{3,2},{5,4},{6,5},{7,6},{9,8},{10,9},{11,10},{13,12},{... | collective-permute-start | bytes 24584 | tf_op jit(solution)/shard_map/ppermute | solution.py:19
  150.9 7.1 %collective-permute-start.18 = (f32[1,2,1,1024]{3,2,1,0:T(1,128)S(1)}, f32[1,2,1,1024]{3,2,1,0:T(1,128)S(1)}, u32[]{:S(2)}, u32[]{:S(2)}) collective-permute-start(f32[1,2,1,1024]{3,2,1,0:T(1,128)S(1)} %get-tuple-element.29), channel_id=1, source_target_pairs={{0,1},{1,2},{2,3},{4,5},{5,6},{6,7},{8,9},{9,10},{10,11},{12,13},{... | collective-permute-start | bytes 24584 | tf_op jit(solution)/shard_map/ppermute | solution.py:16
where the time goes:
time: 191 us; the launch traced here: 190 us
  blocking collectives  77.6 us (41%)
  starting transfers between devices  60.2 us (32%)
  other arithmetic  15.9 us (8%)
  matrix products  13.9 us (7%)
  local copies, waits for them, and re-layouts  11.8 us (6%)
  between operations  10.6 us (6%)
    all_to_all x6, blocking collectives, sent_to_all(): lax.all_to_all(jnp.broadcast_to(x[None], (devices, *x.shape)), axis, 0, 0...  77.6 us
    ppermute x7, starting transfers between devices, passed_along(): return lax.ppermute(x, axis, pairs)  28.6 us
    ppermute x6, starting transfers between devices, extended(): lax.ppermute(lax.slice_in_dim(block, block.shape[dim] - width, None, axis...  23.9 us
    ppermute x6, starting transfers between devices, extended(): lax.ppermute(lax.slice_in_dim(block, 0, width, axis=dim), axis, backward)  7.75 us
    dot_general x3, matrix products, observe(): jnp.einsum('bjc,bc->bj', cell_hot, picked, precision=lax.Precision.HIGHEST)  5.99 us
    reduce_sum x3, other arithmetic, two_products(): jnp.sum(vector * vector)  5.65 us
    mul x3, other arithmetic, backward(): coeffs[3] * state  4.68 us
    dot_general x3, matrix products, observe(): jnp.einsum('bjc,bj->bc', cell_hot, weighted, precision=lax.Precision.HIGH...  4.39 us
  transfers between devices with their start and end apart: 19, of which 0 were waited for; matrix products, arithmetic and copies ran while one was open for 11% of the time, Pallas kernels for 0%

commit v1 on v0

v1 whole, which is shorter than its diff:
```python
import jax
import jax.numpy as jnp
from jax import lax
from jax.experimental import pallas as pl
from jax.experimental.pallas import tpu as pltpu
from jax.sharding import Mesh
from jax.sharding import PartitionSpec as P

WIN = ("win_0", "win_1", "win_2")
THETA = 6.0
G = 8
HALO = 6
F32 = jnp.float32


def call(body, out_shape, aliases=None, smem=(), count=0, scratch=()):
    specs = [
        pl.BlockSpec(memory_space=pltpu.SMEM if i in smem else pltpu.VMEM) for i in range(count)
    ]
    outs = [pl.BlockSpec(memory_space=pltpu.VMEM) for _ in out_shape]
    return pl.pallas_call(
        body,
        out_shape=out_shape,
        in_specs=specs,
        out_specs=outs,
        scratch_shapes=scratch,
        input_output_aliases=aliases or {},
        compiler_params=pltpu.CompilerParams(vmem_limit_bytes=24 * 2**20),
    )


def shape(*dims):
    return jax.ShapeDtypeStruct(dims, F32)


def west(x):
    return pltpu.roll(x, 1, axis=1)


def east(x):
    return pltpu.roll(x, x.shape[1] - 1, axis=1)


def north_of(ref, lev, tile):
    if tile == 0:
        return pltpu.roll(ref[lev, 0:8, :], 1, axis=0)
    return ref[lev, 8 * tile - 1 : 8 * tile + 7, :]


def south_of(ref, lev, tile, tiles):
    if tile == tiles - 1:
        return pltpu.roll(ref[lev, 8 * tile : 8 * tile + 8, :], 7, axis=0)
    return ref[lev, 8 * tile + 1 : 8 * tile + 9, :]


def folded(x):
    total = x[:, 0:128]
    for at in range(128, x.shape[1], 128):
        total = total + x[:, at : at + 128]
    return total


PARTS = (("b", HALO), ("c", HALO - 1), ("w", HALO - 1), ("d", HALO - 2))
PER_LEVEL = HALO + 5 * (HALO - 1) + (HALO - 2)


def message_rows(levels):
    return -(-levels * PER_LEVEL // 8) * 8


def ghost_items(levels):
    at = 0
    for lev in range(levels):
        for name, rows in PARTS:
            for f in range(4 if name == "c" else 1):
                yield name, f, lev, at, rows
                at += rows


def pack_kernel(b, c, w, pos, block, weight, north, south, d, blocks):
    levels, rows, width = b.shape
    per_row = width // 128
    pos_all, weight_all = pos[...], weight[...]
    n = pos_all.shape[0]
    cell = lax.broadcasted_iota(jnp.int32, (n, 128), 1)
    sums = [jnp.zeros((n, 128), F32) for _ in range(4)]
    for j in range(pos_all.shape[1]):
        here = jnp.broadcast_to(pos_all[:, j : j + 1], (n, 128))
        value = jnp.broadcast_to(weight_all[:, j : j + 1], (n, 128))
        sums[j % 4] = sums[j % 4] + jnp.where(here == cell, value, 0.0)
    hot = (sums[0] + sums[1]) + (sums[2] + sums[3])
    blocks[...] = jnp.zeros(blocks.shape, F32)
    for i in range(n):
        at = pl.ds(block[0, i], 1)
        blocks[at, :] = blocks[at, :] + hot[i : i + 1, :]
    for j in range(per_row):
        d[:, j * 128 : j * 128 + 128] = blocks[pl.ds(j, levels * rows, stride=per_row), :]
    for name, f, lev, at, count in ghost_items(levels):
        for out, first in ((north, 0), (south, rows - count)):
            if name == "d":
                piece = d[lev * rows + first : lev * rows + first + count, :]
            elif name == "c":
                piece = c[f, lev, first : first + count, :]
            else:
                piece = (b if name == "b" else w)[lev, first : first + count, :]
            out[at : at + count, :] = piece
    used = levels * PER_LEVEL
    for out in (north, south):
        if out.shape[0] > used:
            out[used:, :] = jnp.zeros((out.shape[0] - used, width), F32)


def extend_kernel(b, c, w, d, b_e, c_e, w_e, d_e):
    levels, rows, width = b.shape
    blank = jnp.zeros((G, width), F32)
    for lev in range(levels):
        targets = [(b_e.at[lev], b.at[lev]), (w_e.at[lev], w.at[lev])]
        targets += [(c_e.at[f, lev], c.at[f, lev]) for f in range(4)]
        targets += [(d_e.at[lev], d.at[lev * rows : (lev + 1) * rows])]
        for out, src in targets:
            out[0:G, :] = blank
            out[G : G + rows, :] = src[...]
            out[G + rows :, :] = blank


def model_tile(q, c, lev, tile, tiles):
    here = q[lev, 8 * tile : 8 * tile + 8, :]
    at = slice(8 * tile, 8 * tile + 8)
    return (
        c[0, lev, at, :] * here
        + c[1, lev, at, :] * (north_of(q, lev, tile) + south_of(q, lev, tile, tiles))
        + c[2, lev, at, :] * east(here)
        + c[3, lev, at, :] * west(here)
    )


def propagate(q, c, p):
    levels, rows, _ = q.shape
    for lev in range(levels):
        for tile in range(rows // 8):
            p[lev, 8 * tile : 8 * tile + 8, :] = model_tile(q, c, lev, tile, rows // 8)


def post(out, values, lev):
    rows = out.shape[1]
    out[lev, :, :] = values[lev, 4 : 4 + rows, :]


def core_is_one():
    return lax.axis_index("win_2") == 1


def ghosts_kernel(from_north, from_south, b_in, c_in, w_in, d_in, b_e, c_e, w_e, d_e, p, cross, within):
    levels, total, width = b_e.shape
    rows = total - 2 * G
    for name, f, lev, at, count in ghost_items(levels):
        out = {"b": b_e, "w": w_e, "d": d_e}.get(name)
        out = c_e.at[f] if out is None else out
        out[lev, G - count : G, :] = from_north[at : at + count, :]
        out[lev, G + rows : G + rows + count, :] = from_south[at : at + count, :]
    propagate(b_e, c_e, p)

    def send(forward, backward):
        for lev in range(levels):
            post(forward, p, lev)
            for f, field in enumerate((b_e, w_e)):
                backward[lev, 16 * f : 16 * f + 8, :] = field[lev, 0:8, :]
                backward[lev, 16 * f + 8 : 16 * f + 16, :] = field[lev, G + rows :, :]
            backward[lev, 32:40, :] = jnp.zeros((8, width), F32)

    @pl.when(core_is_one())
    def _():
        send(cross, within)

    @pl.when(jnp.logical_not(core_is_one()))
    def _():
        send(within, cross)


def unposted(ref, lev, tile, tiles):
    if tile == 0:
        return pltpu.roll(ref[lev, 0:8, :], 4, axis=0)
    if tile == tiles - 1:
        return pltpu.roll(ref[lev, 8 * tile - 8 : 8 * tile, :], 4, axis=0)
    return ref[lev, 8 * tile - 4 : 8 * tile + 4, :]


def second_half(q, c, w, d, p, v_next, w_next, p_prev, out, edge):
    levels, total, _ = q.shape
    tiles = total // 8
    for lev in range(levels):
        for tile in range(tiles):
            at = slice(8 * tile, 8 * tile + 8)
            here, weight = q[lev, at, :], w[lev, at, :]
            following = w_next(lev, tile) * (v_next(lev, tile) - p[lev, at, :])
            edge[lev, at, :] = c[1, lev, at, :] * following
            out[lev, at, :] = (
                (weight + d[lev, at, :] - THETA) * here
                - weight * p_prev(lev, tile)
                - c[0, lev, at, :] * following
                - west(c[2, lev, at, :] * following)
                - east(c[3, lev, at, :] * following)
            )
    for lev in range(levels):
        for tile in range(tiles):
            at = slice(8 * tile, 8 * tile + 8)
            value = out[lev, at, :] - (north_of(edge, lev, tile) + south_of(edge, lev, tile, tiles))
            if tile in (0, tiles - 1):
                value = jnp.where(w[lev, at, :] > 0.0, value, 0.0)
            out[lev, at, :] = value


def products(pairs, levels, tiles, out):
    for i, (x, y) in enumerate(pairs):
        total = jnp.zeros((8, 128), F32)
        for lev in range(levels):
            for tile in range(1, tiles - 1):
                at = slice(8 * tile, 8 * tile + 8)
                total = total + folded(x[lev, at, :] * y[lev, at, :])
        out[i] = total


def send_both(q, p, cross, within):
    def send(forward, backward):
        for lev in range(q.shape[0]):
            post(forward, p, lev)
            post(backward, q, lev)

    @pl.when(core_is_one())
    def _():
        send(cross, within)

    @pl.when(jnp.logical_not(core_is_one()))
    def _():
        send(within, cross)


def first_apply_kernel(
    b_e, c, w, d, p0, b_next, w_next_own, cross_in, within_in,
    q1, p1, w_next, cross, within, sums, edge,
):
    levels, total, width = b_e.shape
    tiles = total // 8
    one = core_is_one()

    def edge_tile(f, lev, tile):
        at = 16 * f + (0 if tile == 0 else 8)
        return jnp.where(one, cross_in[lev, at : at + 8, :], within_in[lev, at : at + 8, :])

    for lev in range(levels):
        for tile in range(tiles):
            at = slice(8 * tile, 8 * tile + 8)
            if tile in (0, tiles - 1):
                w_next[lev, at, :] = edge_tile(1, lev, tile)
            else:
                w_next[lev, at, :] = w_next_own[lev, 8 * tile - G : 8 * tile - G + 8, :]

    def v_next(lev, tile):
        if tile in (0, tiles - 1):
            return edge_tile(0, lev, tile)
        return b_next[lev, 8 * tile - G : 8 * tile - G + 8, :]

    def p_prev(lev, tile):
        return jnp.where(
            one, unposted(within_in, lev, tile, tiles), unposted(cross_in, lev, tile, tiles)
        )

    second_half(
        b_e, c, w, d, p0, v_next,
        lambda lev, tile: w_next[lev, 8 * tile : 8 * tile + 8, :], p_prev, q1, edge,
    )
    propagate(q1, c, p1)
    send_both(q1, p1, cross, within)
    products(((b_e, b_e), (b_e, q1), (q1, q1)), levels, tiles, sums)


def apply_kernel(
    q1, c, w, d, p1, w_next, cross_in, within_in, q2, p2, cross, within, sums, edge
):
    levels, total, width = q1.shape
    tiles = total // 8
    one = core_is_one()

    def v_next(lev, tile):
        return jnp.where(
            one, unposted(cross_in, lev, tile, tiles), unposted(within_in, lev, tile, tiles)
        )

    def p_prev(lev, tile):
        return jnp.where(
            one, unposted(within_in, lev, tile, tiles), unposted(cross_in, lev, tile, tiles)
        )

    second_half(
        q1, c, w, d, p1, v_next,
        lambda lev, tile: w_next[lev, 8 * tile : 8 * tile + 8, :], p_prev, q2, edge,
    )
    propagate(q2, c, p2)
    send_both(q2, p2, cross, within)
    products(((q1, q2), (q2, q2)), levels, tiles, sums)


def moments_kernel(q2, c, w, d, p2, w_next, cross_in, within_in, sums_1, sums_2, out, q3, edge):
    levels, total, width = q2.shape
    tiles = total // 8
    one = core_is_one()
    first = jnp.logical_and(
        lax.axis_index("win_0") + lax.axis_index("win_1") == 0, jnp.logical_not(one)
    )

    def v_next(lev, tile):
        return jnp.where(
            one, unposted(cross_in, lev, tile, tiles), unposted(within_in, lev, tile, tiles)
        )

    def p_prev(lev, tile):
        return jnp.where(
            one, unposted(within_in, lev, tile, tiles), unposted(cross_in, lev, tile, tiles)
        )

    last = jnp.zeros((8, 128), F32)
    for lev in range(levels):
        for tile in range(1, tiles - 1):
            at = slice(8 * tile, 8 * tile + 8)
            here = q2[lev, at, :]
            gap = v_next(lev, tile) - p2[lev, at, :]
            own = d[lev, at, :] - THETA + jnp.where(first, w[lev, at, :], 0.0)
            last = last + folded(w_next[lev, at, :] * gap * gap + own * here * here)
    row = lax.broadcasted_iota(jnp.int32, (8, 128), 0)
    result = jnp.zeros((8, 128), F32)
    for i, part in enumerate([sums_1[0], sums_1[1], sums_1[2], sums_2[0], sums_2[1], last]):
        total_i = jnp.sum(part, axis=0, keepdims=True)
        result = jnp.where(row == i, jnp.broadcast_to(total_i, (8, 128)), result)
    for i in range(out.shape[0]):
        out[i] = result
    second_half(
        q2, c, w, d, p2, v_next,
        lambda lev, tile: w_next[lev, 8 * tile : 8 * tile + 8, :], p_prev, q3, edge,
    )


def spread_kernel(x, out):
    total = x[0]
    for i in range(1, x.shape[0]):
        total = total + x[i]
    for i in range(out.shape[0]):
        out[i] = total


def times_a(v):
    longer = [THETA * x for x in v] + [0.0]
    return [longer[i] + (v[i - 1] if i else 0.0) for i in range(len(longer))]


def inner(u, v, mu):
    return sum(x * y * mu[i + j] for i, x in enumerate(u) for j, y in enumerate(v))


def plus(u, scale, v):
    size = max(len(u), len(v))
    u, v = u + [0.0] * (size - len(u)), v + [0.0] * (size - len(v))
    return [x + scale * y for x, y in zip(u, v)]


def coordinates(mu, iters=3):
    x, r, p = [0.0], [1.0], [1.0]
    rr = mu[0]
    for i in range(iters):
        image = times_a(p)
        alpha = rr / inner(p, image, mu)
        x = plus(x, alpha, p)
        r = plus(r, -alpha, image)
        if i + 1 < iters:
            new = inner(r, r, mu)
            p = plus(r, new / rr, p)
            rr = new
    return x, r


def finish_kernel(parts, q0, q1, q2, q3, solution_field, residual):
    levels, rows, width = solution_field.shape
    total = parts[0]
    for i in range(1, parts.shape[0]):
        total = total + parts[i]
    summed = jnp.sum(total, axis=1, keepdims=True)
    mu = [jnp.broadcast_to(summed[i : i + 1, :], (8, 128)) for i in range(6)]
    x, r = coordinates(mu)
    wide = lambda v: jnp.concatenate([v] * (width // 128), axis=1)
    x = [wide(v) for v in x]
    r = [wide(v) for v in r]
    for lev in range(levels):
        for at in range(0, rows, 8):
            s = [q[lev, G + at : G + at + 8, :] for q in (q0, q1, q2, q3)]
            solution_field[lev, at : at + 8, :] = x[0] * s[0] + x[1] * s[1] + x[2] * s[2]
            residual[lev, at : at + 8, :] = r[0] * s[0] + r[1] * s[1] + r[2] * s[2] + r[3] * s[3]


def shifted(x, axis, by):
    count = lax.axis_size(axis)
    return lax.ppermute(x, axis, [(i, i + by) for i in range(count) if 0 <= i + by < count])


def over_chips(x):
    count = lax.axis_size(WIN)
    pairs = [(i, i + 1) for i in range(1, count - 1, 2)]
    return lax.ppermute(x, WIN, pairs + [(b, a) for a, b in pairs])


def on_chip(x):
    return lax.ppermute(x, "win_2", [(0, 1), (1, 0)])


def on_device(right_side, error_weight, coeffs, obs_block, obs_pos, obs_weight):
    b, w, c = right_side[0], error_weight[0], coeffs[:, 0]
    levels, rows, width = b.shape
    total = rows + 2 * G
    field = shape(levels, total, width)
    ghost = shape(message_rows(levels), width)
    message = shape(levels, 40, width)

    north, south, d = call(
        pack_kernel,
        [ghost, ghost, shape(levels * rows, width)],
        smem=(4,),
        count=6,
        scratch=(pltpu.VMEM((b.size // 128, 128), F32),),
    )(b, c, w, obs_pos[0], obs_block, obs_weight[0])
    from_south = shifted(north, "tile", -1)
    from_north = shifted(south, "tile", 1)
    b_next = shifted(b, WIN, -1)
    w_next_own = shifted(w, WIN, -1)
    b_e, c_e, w_e, d_e = call(
        extend_kernel, [field, shape(4, levels, total, width), field, field], count=4
    )(b, c, w, d)
    b_e, c_e, w_e, d_e, p0, cross, within = call(
        ghosts_kernel,
        [field, shape(4, levels, total, width), field, field, field, message, message],
        aliases={2: 0, 3: 1, 4: 2, 5: 3},
        count=6,
    )(from_north, from_south, b_e, c_e, w_e, d_e)
    cross, within = over_chips(cross), on_chip(within)
    scratch = (pltpu.VMEM((levels, total, width), F32),)
    q1, p1, w_next, cross, within, sums_1 = call(
        first_apply_kernel,
        [field, field, field, message, message, shape(3, 8, 128)],
        count=9,
        scratch=scratch,
    )(b_e, c_e, w_e, d_e, p0, b_next, w_next_own, cross, within)
    cross, within = over_chips(cross), on_chip(within)
    q2, p2, cross, within, sums_2 = call(
        apply_kernel,
        [field, field, message, message, shape(2, 8, 128)],
        count=8,
        scratch=scratch,
    )(q1, c_e, w_e, d_e, p1, w_next, cross, within)
    cross, within = over_chips(cross), on_chip(within)
    near, far = ("win_2", "tile"), ("win_0", "win_1")
    moments, q3 = call(
        moments_kernel, [shape(lax.axis_size(near), 8, 128), field], count=10, scratch=scratch
    )(q2, c_e, w_e, d_e, p2, w_next, cross, within, sums_1, sums_2)
    moments = lax.all_to_all(moments, near, 0, 0, tiled=True)
    (moments,) = call(spread_kernel, [shape(lax.axis_size(far), 8, 128)], count=1)(moments)
    moments = lax.all_to_all(moments, far, 0, 0, tiled=True)
    solution_field, residual = call(
        finish_kernel, [shape(levels, rows, width), shape(levels, rows, width)], count=5
    )(moments, b_e, q1, q2, q3)
    return solution_field[None], residual[None]


def solution(mesh):
    split = Mesh(
        mesh.devices.reshape(8, 8, 2, mesh.shape["tile"]), ("win_0", "win_1", "win_2", "tile")
    )
    in_specs = (
        P(WIN, None, "tile", None),
        P(WIN, None, "tile", None),
        P(None, WIN, None, "tile", None),
        P(WIN, "tile"),
        P(WIN, "tile", None),
        P(WIN, "tile", None),
    )
    out_specs = (P(WIN, None, "tile", None), P(WIN, None, "tile", None))
    return jax.shard_map(
        on_device, mesh=split, in_specs=in_specs, out_specs=out_specs, check_vma=False
    )
```

time: 191 us -> 105 us (0.55)
  starting transfers between devices: 60.2 us -> 26.1 us
  blocking collectives: 77.6 us -> 43.7 us
  waiting for transfers between devices: 0.08 us -> 21.2 us
  other arithmetic: 15.9 us -> 0 us
  matrix products: 13.9 us -> 0 us
  between operations: 10.6 us -> 0.77 us
  local copies, waits for them, and re-layouts: 11.8 us -> 5.21 us
  Pallas kernels: 0 us -> 6.47 us
    ppermute x19 -> x10, starting transfers between devices: 60.2 us -> 26.1 us  [the longest x3 10.8 us: over_chips(): return lax.ppermute(x, WIN, pairs + [(b, a) for a, b in pairs])]
    all_to_all x6 -> x2, blocking collectives: 77.6 us -> 43.7 us  [the longest x1 34.9 us: on_device(): moments = lax.all_to_all(moments, far, 0, 0, tiled=True)]
    ppermute x19 -> x10, waiting for transfers between devices: 0.08 us -> 21.2 us  [the longest x4 12.1 us: shifted(): lax.ppermute(x, axis, [(i, i + by) for i in range(count) if 0 <= i + by <...]
    dot_general x12 -> x0, matrix products: 13.9 us -> none  [the longest x3 5.99 us: observe(): jnp.einsum('bjc,bc->bj', cell_hot, picked, precision=lax.Precision.HIGHEST)]
    pallas_call x0 -> x8, Pallas kernels: none -> 6.47 us  [the longest x1 2.09 us: on_device(): call(pack_kernel, [ghost, ghost, shape(levels * rows, width)], smem=(4,),...]
    reduce_sum x9 -> x0, other arithmetic: 5.98 us -> none  [the longest x3 5.65 us: two_products(): jnp.sum(vector * vector)]
    slice x24 -> x0, local copies, waits for them, and re-layouts: 5.74 us -> none  [the longest x6 2.38 us: forward(): jnp.roll(state, -1, axis=3)]
    mul x9 -> x0, other arithmetic: 4.86 us -> none  [the longest x3 4.68 us: backward(): coeffs[3] * state]
  transfers between devices with their start and end apart: 19 -> 10, of which waited for: 0 -> 6; matrix products, arithmetic and copies ran while one was open for 11% -> 0% of each run, Pallas kernels for 0% -> 0%
where the time goes in v1:
time: 105 us; the launch traced here: 103 us
  blocking collectives  43.7 us (42%)
  starting transfers between devices  26.1 us (25%)
  waiting for transfers between devices  21.2 us (20%)
  Pallas kernels  6.47 us (6%)
  local copies, waits for them, and re-layouts  5.21 us (5%)
    all_to_all x1, blocking collectives, on_device(): moments = lax.all_to_all(moments, far, 0, 0, tiled=True)  34.9 us
    ppermute x4, waiting for transfers between devices, shifted(): lax.ppermute(x, axis, [(i, i + by) for i in range(count) if 0 <= i + by <...  12.1 us
    ppermute x3, starting transfers between devices, over_chips(): return lax.ppermute(x, WIN, pairs + [(b, a) for a, b in pairs])  10.8 us
    ppermute x4, starting transfers between devices, shifted(): lax.ppermute(x, axis, [(i, i + by) for i in range(count) if 0 <= i + by <...  9.57 us
    ppermute x3, waiting for transfers between devices, over_chips(): return lax.ppermute(x, WIN, pairs + [(b, a) for a, b in pairs])  9.07 us
    all_to_all x1, blocking collectives, on_device(): moments = lax.all_to_all(moments, near, 0, 0, tiled=True)  8.83 us
    ppermute x3, starting transfers between devices, on_chip(): return lax.ppermute(x, 'win_2', [(0, 1), (1, 0)])  5.76 us
    unnamed x12, local copies, waits for them, and re-layouts  5.21 us
  transfers between devices with their start and end apart: 10, of which 6 were waited for; matrix products, arithmetic and copies ran while one was open for 0% of the time, Pallas kernels for 0%

profile of v1, /device:TPU:1, one launch (start us, length us, event | category | flops | bytes accessed | tf_op | source)
XLA Modules:
  0.0 103.5 jit_solution(7386240915867832069)
XLA Ops:
  0.6 1.2 %copy-done = f32[4,1,2,32,1024]{4,3,2,1,0:T(8,128)S(1)} copy-done((f32[4,1,2,32,1024]{4,3,2,1,0:T(8,128)S(1)}, f32[4,1,2,32,1024]{4,3,2,1,0:T(8,128)}, u32[]{:S(2)}) %copy-start) | copy-done | bytes 1048600
  1.9 0.9 copy-done.1
  2.8 0.9 copy-done.2
  3.8 0.7 copy-done.3
  4.5 0.7 copy-done.4
  5.2 0.7 copy-done.5
  5.8 2.1 %shard_map.77 = (f32[72,1024]{1,0:T(8,128)S(1)}, f32[72,1024]{1,0:T(8,128)S(1)}, f32[64,1024]{1,0:T(8,128)S(1)}) custom-call(f32[2,32,1024]{2,1,0:T(8,128)S(1)} %bitcast.9, f32[4,2,32,1024]{3,2,1,0:T(8,128)S(1)} %bitcast.7, f32[2,32,1024]{2,1,0:T(8,128)S(1)} %bitcast.12, s32[32,128]{1,0:T(8,128)S(1)} %bitcast.15, s32[1,32]{1,0:T(1,128)S(1)} %copy-done.5, ...), custom_call_target="tpu_custom_call" | custom-call | tf_op jit(solution)/shard_map/pallas_call | solution.py:421
  7.9 4.0 %collective-permute-start = (f32[72,1024]{1,0:T(8,128)S(1)}, f32[72,1024]{1,0:T(8,128)S(1)}, u32[]{:S(2)}, u32[]{:S(2)}) collective-permute-start(f32[72,1024]{1,0:T(8,128)S(1)} %get-tuple-element.31), channel_id=1, source_target_pairs={{0,1},{1,2},{2,3},{4,5},{5,6},{6,7},{8,9},{9,10},{10,11},{12,13},{... | collective-permute-start | bytes 884744 | tf_op jit(solution)/shard_map/ppermute | solution.py:400
  11.9 1.3 %collective-permute-start.1 = (f32[72,1024]{1,0:T(8,128)S(1)}, f32[72,1024]{1,0:T(8,128)S(1)}, u32[]{:S(2)}, u32[]{:S(2)}) collective-permute-start(f32[72,1024]{1,0:T(8,128)S(1)} %get-tuple-element.32), channel_id=1, source_target_pairs={{1,0},{2,1},{3,2},{5,4},{6,5},{7,6},{9,8},{10,9},{11,10},{13,12},{... | collective-permute-start | bytes 884744 | tf_op jit(solution)/shard_map/ppermute | solution.py:400
  13.2 0.2 shard_map.78
  13.4 2.1 %collective-permute-done.from_north = f32[72,1024]{1,0:T(8,128)S(1)} collective-permute-done((f32[72,1024]{1,0:T(8,128)S(1)}, f32[72,1024]{1,0:T(8,128)S(1)}, u32[]{:S(2)}, u32[]{:S(2)}) %collective-permute-start) | collective-permute-done | bytes 294944 | tf_op jit(solution)/shard_map/ppermute | solution.py:400
  15.5 3.8 %collective-permute-done.1.from_south = f32[72,1024]{1,0:T(8,128)S(1)} collective-permute-done((f32[72,1024]{1,0:T(8,128)S(1)}, f32[72,1024]{1,0:T(8,128)S(1)}, u32[]{:S(2)}, u32[]{:S(2)}) %collective-permute-start.1) | collective-permute-done | bytes 294944 | tf_op jit(solution)/shard_map/ppermute | solution.py:400
  19.4 0.4 shard_map.79
  19.8 6.9 %collective-permute-start.4 = (f32[2,40,1024]{2,1,0:T(8,128)S(1)}, f32[2,40,1024]{2,1,0:T(8,128)S(1)}, u32[]{:S(2)}, u32[]{:S(2)}) collective-permute-start(f32[2,40,1024]{2,1,0:T(8,128)S(1)} %get-tuple-element.43), channel_id=1, source_target_pairs={{4,8},{12,16},{20,24},{28,32},{36,40},{44,48},{52,56},{60,64},{68,... | collective-permute-start | bytes 983048 | tf_op jit(solution)/shard_map/ppermute | solution.py:406
  26.7 1.9 %collective-permute-start.5 = (f32[2,40,1024]{2,1,0:T(8,128)S(1)}, f32[2,40,1024]{2,1,0:T(8,128)S(1)}, u32[]{:S(2)}, u32[]{:S(2)}) collective-permute-start(f32[2,40,1024]{2,1,0:T(8,128)S(1)} %get-tuple-element.44), channel_id=1, source_target_pairs={{0,4},{4,0},{1,5},{5,1},{2,6},{6,2},{3,7},{7,3},{8,12},{12,8},{9,1... | collective-permute-start | bytes 983048 | tf_op jit(solution)/shard_map/ppermute | solution.py:410
  28.7 2.4 %collective-permute-start.2 = (f32[2,32,1024]{2,1,0:T(8,128)S(1)}, f32[2,32,1024]{2,1,0:T(8,128)S(1)}, u32[]{:S(2)}, u32[]{:S(2)}) collective-permute-start(f32[2,32,1024]{2,1,0:T(8,128)S(1)} %bitcast.11), channel_id=1, source_target_pairs={{4,0},{8,4},{12,8},{16,12},{20,16},{24,20},{28,24},{32,28},{36,32}... | collective-permute-start | bytes 786440 | tf_op jit(solution)/shard_map/ppermute | solution.py:400
  31.1 1.9 %collective-permute-start.3 = (f32[2,32,1024]{2,1,0:T(8,128)S(1)}, f32[2,32,1024]{2,1,0:T(8,128)S(1)}, u32[]{:S(2)}, u32[]{:S(2)}) collective-permute-start(f32[2,32,1024]{2,1,0:T(8,128)S(1)} %bitcast.14), channel_id=1, source_target_pairs={{4,0},{8,4},{12,8},{16,12},{20,16},{24,20},{28,24},{32,28},{36,32}... | collective-permute-start | bytes 786440 | tf_op jit(solution)/shard_map/ppermute | solution.py:400
  33.0 3.3 %collective-permute-done.2.b_next = f32[2,32,1024]{2,1,0:T(8,128)S(1)} collective-permute-done((f32[2,32,1024]{2,1,0:T(8,128)S(1)}, f32[2,32,1024]{2,1,0:T(8,128)S(1)}, u32[]{:S(2)}, u32[]{:S(2)}) %collective-permute-start.2) | collective-permute-done | bytes 262176 | tf_op jit(solution)/shard_map/ppermute | solution.py:400
  36.4 2.8 %collective-permute-done.3.w_next_own = f32[2,32,1024]{2,1,0:T(8,128)S(1)} collective-permute-done((f32[2,32,1024]{2,1,0:T(8,128)S(1)}, f32[2,32,1024]{2,1,0:T(8,128)S(1)}, u32[]{:S(2)}, u32[]{:S(2)}) %collective-permute-start.3) | collective-permute-done | bytes 262176 | tf_op jit(solution)/shard_map/ppermute | solution.py:400
  39.2 0.0 collective-permute-done.4.cross_in
  39.2 0.9 shard_map.80
  40.1 1.9 %collective-permute-start.6 = (f32[2,40,1024]{2,1,0:T(8,128)S(1)}, f32[2,40,1024]{2,1,0:T(8,128)S(1)}, u32[]{:S(2)}, u32[]{:S(2)}) collective-permute-start(f32[2,40,1024]{2,1,0:T(8,128)S(1)} %get-tuple-element.48), channel_id=1, source_target_pairs={{4,8},{12,16},{20,24},{28,32},{36,40},{44,48},{52,56},{60,64},{68,... | collective-permute-start | bytes 983048 | tf_op jit(solution)/shard_map/ppermute | solution.py:406
  42.0 1.9 %collective-permute-start.7 = (f32[2,40,1024]{2,1,0:T(8,128)S(1)}, f32[2,40,1024]{2,1,0:T(8,128)S(1)}, u32[]{:S(2)}, u32[]{:S(2)}) collective-permute-start(f32[2,40,1024]{2,1,0:T(8,128)S(1)} %get-tuple-element.49), channel_id=1, source_target_pairs={{0,4},{4,0},{1,5},{5,1},{2,6},{6,2},{3,7},{7,3},{8,12},{12,8},{9,1... | collective-permute-start | bytes 983048 | tf_op jit(solution)/shard_map/ppermute | solution.py:410
  44.0 4.5 %collective-permute-done.6.cross_in = f32[2,40,1024]{2,1,0:T(8,128)S(1)} collective-permute-done((f32[2,40,1024]{2,1,0:T(8,128)S(1)}, f32[2,40,1024]{2,1,0:T(8,128)S(1)}, u32[]{:S(2)}, u32[]{:S(2)}) %collective-permute-start.6) | collective-permute-done | bytes 327712 | tf_op jit(solution)/shard_map/ppermute | solution.py:406
  48.5 1.0 shard_map.81
  49.5 1.9 %collective-permute-start.8 = (f32[2,40,1024]{2,1,0:T(8,128)S(1)}, f32[2,40,1024]{2,1,0:T(8,128)S(1)}, u32[]{:S(2)}, u32[]{:S(2)}) collective-permute-start(f32[2,40,1024]{2,1,0:T(8,128)S(1)} %get-tuple-element.52), channel_id=1, source_target_pairs={{4,8},{12,16},{20,24},{28,32},{36,40},{44,48},{52,56},{60,64},{68,... | collective-permute-start | bytes 983048 | tf_op jit(solution)/shard_map/ppermute | solution.py:406
  51.4 1.9 %collective-permute-start.9 = (f32[2,40,1024]{2,1,0:T(8,128)S(1)}, f32[2,40,1024]{2,1,0:T(8,128)S(1)}, u32[]{:S(2)}, u32[]{:S(2)}) collective-permute-start(f32[2,40,1024]{2,1,0:T(8,128)S(1)} %get-tuple-element.53), channel_id=1, source_target_pairs={{0,4},{4,0},{1,5},{5,1},{2,6},{6,2},{3,7},{7,3},{8,12},{12,8},{9,1... | collective-permute-start | bytes 983048 | tf_op jit(solution)/shard_map/ppermute | solution.py:410
  53.3 4.5 %collective-permute-done.8.cross_in = f32[2,40,1024]{2,1,0:T(8,128)S(1)} collective-permute-done((f32[2,40,1024]{2,1,0:T(8,128)S(1)}, f32[2,40,1024]{2,1,0:T(8,128)S(1)}, u32[]{:S(2)}, u32[]{:S(2)}) %collective-permute-start.8) | collective-permute-done | bytes 327712 | tf_op jit(solution)/shard_map/ppermute | solution.py:406
  57.9 0.8 shard_map.82
  58.6 8.8 %all_to_all.10.x = f32[8,8,128]{2,1,0:T(8,128)S(1)} all-to-all(f32[8,8,128]{2,1,0:T(8,128)S(1)} %get-tuple-element.56), channel_id=1, replica_groups=mesh['win_0'=8,'win_1'=8,'win_2'=2,'tile'=4] {'win_2','tile'}, dimensions={0} | all-to-all | bytes 65536 | tf_op jit(solution)/shard_map/all_to_all | solution.py:461
  67.5 34.9 %all_to_all.11.parts = f32[64,8,128]{2,1,0:T(8,128)S(1)} all-to-all(f32[64,8,128]{2,1,0:T(8,128)S(1)} %shard_map.83), channel_id=1, replica_groups=mesh['win_0'=8,'win_1'=8,'win_2'=2,'tile'=4] {'win_0','win_1'}, dimensions={0} | all-to-all | bytes 524288 | tf_op jit(solution)/shard_map/all_to_all | solution.py:463
  102.4 1.1 %shard_map.84 = (f32[2,32,1024]{2,1,0:T(8,128)}, f32[2,32,1024]{2,1,0:T(8,128)}) custom-call(f32[64,8,128]{2,1,0:T(8,128)S(1)} %all_to_all.11.parts, f32[2,48,1024]{2,1,0:T(8,128)S(1)} %get-tuple-element.38.b_e.q0, f32[2,48,1024]{2,1,0:T(8,128)S(1)} %get-tuple-element.45.q1, f32[2,48,1024]{2,1,0:T(8,128)S(1)} %get-tuple-element.50.q2, ...), custom_call_target="tpu_custom_call" | custom-call | tf_op jit(solution)/shard_map/pallas_call | solution.py:464
  (10 shorter events, 0.0 us)
Async XLA Ops:
  0.6 1.2 %copy-start = (f32[4,1,2,32,1024]{4,3,2,1,0:T(8,128)S(1)}, f32[4,1,2,32,1024]{4,3,2,1,0:T(8,128)}, u32[]{:S(2)}) copy-start(f32[4,1,2,32,1024]{4,3,2,1,0:T(8,128)} %param.8) | copy-start | bytes 3145732
  1.9 0.9 copy-start.1
  2.8 0.9 copy-start.2
  3.8 0.7 copy-start.3
  4.5 0.7 copy-start.4
  5.2 0.7 copy-start.5
  7.9 7.6 %collective-permute-start = (f32[72,1024]{1,0:T(8,128)S(1)}, f32[72,1024]{1,0:T(8,128)S(1)}, u32[]{:S(2)}, u32[]{:S(2)}) collective-permute-start(f32[72,1024]{1,0:T(8,128)S(1)} %get-tuple-element.31), channel_id=1, source_target_pairs={{0,1},{1,2},{2,3},{4,5},{5,6},{6,7},{8,9},{9,10},{10,11},{12,13},{... | collective-permute-start | bytes 884744 | tf_op jit(solution)/shard_map/ppermute | solution.py:400
  11.9 7.5 %collective-permute-start.1 = (f32[72,1024]{1,0:T(8,128)S(1)}, f32[72,1024]{1,0:T(8,128)S(1)}, u32[]{:S(2)}, u32[]{:S(2)}) collective-permute-start(f32[72,1024]{1,0:T(8,128)S(1)} %get-tuple-element.32), channel_id=1, source_target_pairs={{1,0},{2,1},{3,2},{5,4},{6,5},{7,6},{9,8},{10,9},{11,10},{13,12},{... | collective-permute-start | bytes 884744 | tf_op jit(solution)/shard_map/ppermute | solution.py:400
  19.8 19.4 %collective-permute-start.4 = (f32[2,40,1024]{2,1,0:T(8,128)S(1)}, f32[2,40,1024]{2,1,0:T(8,128)S(1)}, u32[]{:S(2)}, u32[]{:S(2)}) collective-permute-start(f32[2,40,1024]{2,1,0:T(8,128)S(1)} %get-tuple-element.43), channel_id=1, source_target_pairs={{4,8},{12,16},{20,24},{28,32},{36,40},{44,48},{52,56},{60,64},{68,... | collective-permute-start | bytes 983048 | tf_op jit(solution)/shard_map/ppermute | solution.py:406
  26.7 12.4 %collective-permute-start.5 = (f32[2,40,1024]{2,1,0:T(8,128)S(1)}, f32[2,40,1024]{2,1,0:T(8,128)S(1)}, u32[]{:S(2)}, u32[]{:S(2)}) collective-permute-start(f32[2,40,1024]{2,1,0:T(8,128)S(1)} %get-tuple-element.44), channel_id=1, source_target_pairs={{0,4},{4,0},{1,5},{5,1},{2,6},{6,2},{3,7},{7,3},{8,12},{12,8},{9,1... | collective-permute-start | bytes 983048 | tf_op jit(solution)/shard_map/ppermute | solution.py:410
  28.7 7.7 %collective-permute-start.2 = (f32[2,32,1024]{2,1,0:T(8,128)S(1)}, f32[2,32,1024]{2,1,0:T(8,128)S(1)}, u32[]{:S(2)}, u32[]{:S(2)}) collective-permute-start(f32[2,32,1024]{2,1,0:T(8,128)S(1)} %bitcast.11), channel_id=1, source_target_pairs={{4,0},{8,4},{12,8},{16,12},{20,16},{24,20},{28,24},{32,28},{36,32}... | collective-permute-start | bytes 786440 | tf_op jit(solution)/shard_map/ppermute | solution.py:400
  31.1 8.1 %collective-permute-start.3 = (f32[2,32,1024]{2,1,0:T(8,128)S(1)}, f32[2,32,1024]{2,1,0:T(8,128)S(1)}, u32[]{:S(2)}, u32[]{:S(2)}) collective-permute-start(f32[2,32,1024]{2,1,0:T(8,128)S(1)} %bitcast.14), channel_id=1, source_target_pairs={{4,0},{8,4},{12,8},{16,12},{20,16},{24,20},{28,24},{32,28},{36,32}... | collective-permute-start | bytes 786440 | tf_op jit(solution)/shard_map/ppermute | solution.py:400
  40.1 8.4 %collective-permute-start.6 = (f32[2,40,1024]{2,1,0:T(8,128)S(1)}, f32[2,40,1024]{2,1,0:T(8,128)S(1)}, u32[]{:S(2)}, u32[]{:S(2)}) collective-permute-start(f32[2,40,1024]{2,1,0:T(8,128)S(1)} %get-tuple-element.48), channel_id=1, source_target_pairs={{4,8},{12,16},{20,24},{28,32},{36,40},{44,48},{52,56},{60,64},{68,... | collective-permute-start | bytes 983048 | tf_op jit(solution)/shard_map/ppermute | solution.py:406
  42.0 6.5 %collective-permute-start.7 = (f32[2,40,1024]{2,1,0:T(8,128)S(1)}, f32[2,40,1024]{2,1,0:T(8,128)S(1)}, u32[]{:S(2)}, u32[]{:S(2)}) collective-permute-start(f32[2,40,1024]{2,1,0:T(8,128)S(1)} %get-tuple-element.49), channel_id=1, source_target_pairs={{0,4},{4,0},{1,5},{5,1},{2,6},{6,2},{3,7},{7,3},{8,12},{12,8},{9,1... | collective-permute-start | bytes 983048 | tf_op jit(solution)/shard_map/ppermute | solution.py:410
  49.5 8.4 %collective-permute-start.8 = (f32[2,40,1024]{2,1,0:T(8,128)S(1)}, f32[2,40,1024]{2,1,0:T(8,128)S(1)}, u32[]{:S(2)}, u32[]{:S(2)}) collective-permute-start(f32[2,40,1024]{2,1,0:T(8,128)S(1)} %get-tuple-element.52), channel_id=1, source_target_pairs={{4,8},{12,16},{20,24},{28,32},{36,40},{44,48},{52,56},{60,64},{68,... | collective-permute-start | bytes 983048 | tf_op jit(solution)/shard_map/ppermute | solution.py:406
  51.4 6.5 %collective-permute-start.9 = (f32[2,40,1024]{2,1,0:T(8,128)S(1)}, f32[2,40,1024]{2,1,0:T(8,128)S(1)}, u32[]{:S(2)}, u32[]{:S(2)}) collective-permute-start(f32[2,40,1024]{2,1,0:T(8,128)S(1)} %get-tuple-element.53), channel_id=1, source_target_pairs={{0,4},{4,0},{1,5},{5,1},{2,6},{6,2},{3,7},{7,3},{8,12},{12,8},{9,1... | collective-permute-start | bytes 983048 | tf_op jit(solution)/shard_map/ppermute | solution.py:410

commit v2 on v1

--- a/solution.py
+++ b/solution.py
@@ -6,6 +6,7 @@
 from jax.sharding import Mesh
 from jax.sharding import PartitionSpec as P
 
+
 WIN = ("win_0", "win_1", "win_2")
 THETA = 6.0
 G = 8
@@ -13,20 +14,21 @@
 F32 = jnp.float32
 
 
-def call(body, out_shape, aliases=None, smem=(), count=0, scratch=()):
-    specs = [
-        pl.BlockSpec(memory_space=pltpu.SMEM if i in smem else pltpu.VMEM) for i in range(count)
-    ]
-    outs = [pl.BlockSpec(memory_space=pltpu.VMEM) for _ in out_shape]
+def call(body, out_shape, aliases=None, hbm=False, count=0, scratch=()):
+    place = pltpu.HBM if hbm else pltpu.VMEM
     return pl.pallas_call(
         body,
         out_shape=out_shape,
-        in_specs=specs,
-        out_specs=outs,
+        in_specs=[pl.BlockSpec(memory_space=place) for _ in range(count)],
+        out_specs=[pl.BlockSpec(memory_space=pltpu.VMEM) for _ in out_shape],
         scratch_shapes=scratch,
         input_output_aliases=aliases or {},
         compiler_params=pltpu.CompilerParams(vmem_limit_bytes=24 * 2**20),
     )
+
+
+def in_hbm(x):
+    return pltpu.with_memory_space_constraint(x, pltpu.HBM)
 
 
 def shape(*dims):
@@ -64,6 +66,9 @@
 PER_LEVEL = HALO + 5 * (HALO - 1) + (HALO - 2)
 
 
+EDGES = 20
+
+
 def message_rows(levels):
     return -(-levels * PER_LEVEL // 8) * 8
 
@@ -77,9 +82,37 @@
                 at += rows
 
 
-def pack_kernel(b, c, w, pos, block, weight, north, south, d, blocks):
-    levels, rows, width = b.shape
+def pack_kernel(
+    b_hbm, c_hbm, w_hbm, pos_hbm, block_hbm, weight_hbm,
+    north, south, b_e, c_e, w_e, d_e, cross, within,
+    pos, block, weight, blocks, sems,
+):
+    levels, rows, width = b_hbm.shape
     per_row = width // 128
+    own = pl.ds(G, rows)
+    moves = [
+        pltpu.make_async_copy(src, dst, sems.at[i])
+        for i, (src, dst) in enumerate(
+            (
+                (pos_hbm, pos),
+                (weight_hbm, weight),
+                (block_hbm, block),
+                (b_hbm, b_e.at[:, own, :]),
+                (c_hbm, c_e.at[:, :, own, :]),
+                (w_hbm, w_e.at[:, own, :]),
+            )
+        )
+    ]
+    for move in moves:
+        move.start()
+    blank = jnp.zeros((G, width), F32)
+    for lev in range(levels):
+        for out in (b_e.at[lev], w_e.at[lev], d_e.at[lev], *(c_e.at[f, lev] for f in range(4))):
+            out[0:G, :] = blank
+            out[G + rows :, :] = blank
+    blocks[...] = jnp.zeros(blocks.shape, F32)
+    for move in moves[:3]:
+        move.wait()
     pos_all, weight_all = pos[...], weight[...]
     n = pos_all.shape[0]
     cell = lax.broadcasted_iota(jnp.int32, (n, 128), 1)
@@ -89,38 +122,41 @@
         value = jnp.broadcast_to(weight_all[:, j : j + 1], (n, 128))
         sums[j % 4] = sums[j % 4] + jnp.where(here == cell, value, 0.0)
     hot = (sums[0] + sums[1]) + (sums[2] + sums[3])
-    blocks[...] = jnp.zeros(blocks.shape, F32)
     for i in range(n):
         at = pl.ds(block[0, i], 1)
         blocks[at, :] = blocks[at, :] + hot[i : i + 1, :]
-    for j in range(per_row):
-        d[:, j * 128 : j * 128 + 128] = blocks[pl.ds(j, levels * rows, stride=per_row), :]
+    for lev in range(levels):
+        for j in range(per_row):
+            first = lev * rows * per_row + j
+            d_e[lev, G : G + rows, j * 128 : j * 128 + 128] = blocks[
+                pl.ds(first, rows, stride=per_row), :
+            ]
+    for move in moves[3:]:
+        move.wait()
     for name, f, lev, at, count in ghost_items(levels):
-        for out, first in ((north, 0), (south, rows - count)):
-            if name == "d":
-                piece = d[lev * rows + first : lev * rows + first + count, :]
-            elif name == "c":
-                piece = c[f, lev, first : first + count, :]
-            else:
-                piece = (b if name == "b" else w)[lev, first : first + count, :]
-            out[at : at + count, :] = piece
+        src = {"b": b_e, "w": w_e, "d": d_e}.get(name)
+        src = c_e.at[f] if src is None else src
+        north[at : at + count, :] = src[lev, G : G + count, :]
+        south[at : at + count, :] = src[lev, G + rows - count : G + rows, :]
     used = levels * PER_LEVEL
     for out in (north, south):
         if out.shape[0] > used:
             out[used:, :] = jnp.zeros((out.shape[0] - used, width), F32)
 
-
-def extend_kernel(b, c, w, d, b_e, c_e, w_e, d_e):
-    levels, rows, width = b.shape
-    blank = jnp.zeros((G, width), F32)
-    for lev in range(levels):
-        targets = [(b_e.at[lev], b.at[lev]), (w_e.at[lev], w.at[lev])]
-        targets += [(c_e.at[f, lev], c.at[f, lev]) for f in range(4)]
-        targets += [(d_e.at[lev], d.at[lev * rows : (lev + 1) * rows])]
-        for out, src in targets:
-            out[0:G, :] = blank
-            out[G : G + rows, :] = src[...]
-            out[G + rows :, :] = blank
+    def send(forward, backward):
+        for lev in range(levels):
+            backward[lev, :, :] = b_e[lev, G : G + rows, :]
+            for tile in range(1, 1 + rows // 8):
+                at = 8 * tile - G
+                forward[lev, at : at + 8, :] = model_tile(b_e, c_e, lev, tile, 2 + rows // 8)
+
+    @pl.when(core_is_one())
+    def _():
+        send(cross, within)
+
+    @pl.when(jnp.logical_not(core_is_one()))
+    def _():
+        send(within, cross)
 
 
 def model_tile(q, c, lev, tile, tiles):
@@ -162,11 +198,14 @@
 
     def send(forward, backward):
         for lev in range(levels):
-            post(forward, p, lev)
-            for f, field in enumerate((b_e, w_e)):
-                backward[lev, 16 * f : 16 * f + 8, :] = field[lev, 0:8, :]
-                backward[lev, 16 * f + 8 : 16 * f + 16, :] = field[lev, G + rows :, :]
-            backward[lev, 32:40, :] = jnp.zeros((8, width), F32)
+            at = lev * EDGES
+            for f, (field, first) in enumerate(((b_e, 3), (w_e, 3))):
+                low, high = at + 10 * f, at + 10 * f + 5
+                backward[low : low + 5, :] = field[lev, first : first + 5, :]
+                backward[high : high + 5, :] = field[lev, G + rows : G + rows + 5, :]
+            forward[at : at + 5, :] = p[lev, 4:9, :]
+            forward[at + 5 : at + 10, :] = p[lev, G + rows - 1 : G + rows + 4, :]
+            forward[at + 10 : at + EDGES, :] = jnp.zeros((EDGES - 10, width), F32)
 
     @pl.when(core_is_one())
     def _():
@@ -236,29 +275,61 @@
 
 
 def first_apply_kernel(
-    b_e, c, w, d, p0, b_next, w_next_own, cross_in, within_in,
-    q1, p1, w_next, cross, within, sums, edge,
+    b_e, c, w, d, p0, cross_own, within_own, w_next_own, cross_in, within_in,
+    q1, p1, w_next, cross, within, sums, edge, v_next, p_prev,
 ):
     levels, total, width = b_e.shape
     tiles = total // 8
+    rows = total - 2 * G
+
+    def assemble(p_own, v_own, p_edges, v_edges):
+        for lev in range(levels):
+            at = lev * EDGES
+            for out, src in ((p_prev, p_own), (v_next, v_own), (w_next, w_next_own)):
+                out[lev, G : G + rows, :] = src[lev, :, :]
+            for f, out in enumerate((v_next, w_next)):
+                low, high = at + 10 * f, at + 10 * f + 5
+                out[lev, 3:8, :] = v_edges[low : low + 5, :]
+                out[lev, G + rows : G + rows + 5, :] = v_edges[high : high + 5, :]
+            p_prev[lev, 4:9, :] = p_edges[at : at + 5, :]
+            p_prev[lev, G + rows - 1 : G + rows + 4, :] = p_edges[at + 5 : at + 10, :]
+
+    blank = jnp.zeros((G, width), F32)
+    for lev in range(levels):
+        for out in (p_prev, v_next, w_next):
+            out[lev, 0:G, :] = blank
+            out[lev, G + rows :, :] = blank
+
+    @pl.when(core_is_one())
+    def _():
+        assemble(within_own, cross_own, within_in, cross_in)
+
+    @pl.when(jnp.logical_not(core_is_one()))
+    def _():
+        assemble(cross_own, within_own, cross_in, within_in)
+
+    def tile_of(ref):
+        return lambda lev, tile: ref[lev, 8 * tile : 8 * tile + 8, :]
+
+    second_half(
+        b_e, c, w, d, p0, tile_of(v_next), tile_of(w_next), tile_of(p_prev), q1, edge
+    )
+    propagate(q1, c, p1)
+    send_both(q1, p1, cross, within)
+    products(((b_e, b_e), (b_e, q1), (q1, q1)), levels, tiles, sums)
+
+
+def apply_kernel(
+    q1, c, w, d, p1, w_next, cross_in, within_in, q2, p2, cross, within, sums, edge
+):
+    levels, total, _ = q1.shape
+    tiles = total // 8
     one = core_is_one()
 
-    def edge_tile(f, lev, tile):
-        at = 16 * f + (0 if tile == 0 else 8)
-        return jnp.where(one, cross_in[lev, at : at + 8, :], within_in[lev, at : at + 8, :])
-
-    for lev in range(levels):
-        for tile in range(tiles):
-            at = slice(8 * tile, 8 * tile + 8)
-            if tile in (0, tiles - 1):
-                w_next[lev, at, :] = edge_tile(1, lev, tile)
-            else:
-                w_next[lev, at, :] = w_next_own[lev, 8 * tile - G : 8 * tile - G + 8, :]
-
     def v_next(lev, tile):
-        if tile in (0, tiles - 1):
-            return edge_tile(0, lev, tile)
-        return b_next[lev, 8 * tile - G : 8 * tile - G + 8, :]
+        return jnp.where(
+            one, unposted(cross_in, lev, tile, tiles), unposted(within_in, lev, tile, tiles)
+        )
 
     def p_prev(lev, tile):
         return jnp.where(
@@ -266,32 +337,6 @@
         )
 
     second_half(
-        b_e, c, w, d, p0, v_next,
-        lambda lev, tile: w_next[lev, 8 * tile : 8 * tile + 8, :], p_prev, q1, edge,
-    )
-    propagate(q1, c, p1)
-    send_both(q1, p1, cross, within)
-    products(((b_e, b_e), (b_e, q1), (q1, q1)), levels, tiles, sums)
-
-
-def apply_kernel(
-    q1, c, w, d, p1, w_next, cross_in, within_in, q2, p2, cross, within, sums, edge
-):
-    levels, total, width = q1.shape
-    tiles = total // 8
-    one = core_is_one()
-
-    def v_next(lev, tile):
-        return jnp.where(
-            one, unposted(cross_in, lev, tile, tiles), unposted(within_in, lev, tile, tiles)
-        )
-
-    def p_prev(lev, tile):
-        return jnp.where(
-            one, unposted(within_in, lev, tile, tiles), unposted(cross_in, lev, tile, tiles)
-        )
-
-    second_half(
         q1, c, w, d, p1, v_next,
         lambda lev, tile: w_next[lev, 8 * tile : 8 * tile + 8, :], p_prev, q2, edge,
     )
@@ -301,7 +346,7 @@
 
 
 def moments_kernel(q2, c, w, d, p2, w_next, cross_in, within_in, sums_1, sums_2, out, q3, edge):
-    levels, total, width = q2.shape
+    levels, total, _ = q2.shape
     tiles = total // 8
     one = core_is_one()
     first = jnp.logical_and(
@@ -400,6 +445,12 @@
     return lax.ppermute(x, axis, [(i, i + by) for i in range(count) if 0 <= i + by < count])
 
 
+def exchanged(cross, within):
+    cross = over_chips(cross)
+    within = on_chip(within)
+    return cross, within
+
+
 def over_chips(x):
     count = lax.axis_size(WIN)
     pairs = [(i, i + 1) for i in range(1, count - 1, 2)]
@@ -410,50 +461,57 @@
     return lax.ppermute(x, "win_2", [(0, 1), (1, 0)])
 
 
-def on_device(right_side, error_weight, coeffs, obs_block, obs_pos, obs_weight):
+def solve(right_side, error_weight, coeffs, obs_block, obs_pos, obs_weight):
     b, w, c = right_side[0], error_weight[0], coeffs[:, 0]
     levels, rows, width = b.shape
     total = rows + 2 * G
     field = shape(levels, total, width)
+    fields = shape(4, levels, total, width)
+    own = shape(levels, rows, width)
     ghost = shape(message_rows(levels), width)
+    edges = shape(levels * EDGES, width)
     message = shape(levels, 40, width)
 
-    north, south, d = call(
+    north, south, b_e, c_e, w_e, d_e, cross_own, within_own = call(
         pack_kernel,
-        [ghost, ghost, shape(levels * rows, width)],
-        smem=(4,),
+        [ghost, ghost, field, fields, field, field, own, own],
+        hbm=True,
         count=6,
-        scratch=(pltpu.VMEM((b.size // 128, 128), F32),),
-    )(b, c, w, obs_pos[0], obs_block, obs_weight[0])
+        scratch=(
+            pltpu.VMEM(obs_pos.shape[1:], jnp.int32),
+            pltpu.SMEM(obs_block.shape, jnp.int32),
+            pltpu.VMEM(obs_weight.shape[1:], F32),
+            pltpu.VMEM((b.size // 128, 128), F32),
+            pltpu.SemaphoreType.DMA((6,)),
+        ),
+    )(*(in_hbm(x) for x in (b, c, w, obs_pos[0], obs_block, obs_weight[0])))
     from_south = shifted(north, "tile", -1)
     from_north = shifted(south, "tile", 1)
-    b_next = shifted(b, WIN, -1)
+    cross_own = over_chips(cross_own)
+    within_own = on_chip(within_own)
     w_next_own = shifted(w, WIN, -1)
-    b_e, c_e, w_e, d_e = call(
-        extend_kernel, [field, shape(4, levels, total, width), field, field], count=4
-    )(b, c, w, d)
     b_e, c_e, w_e, d_e, p0, cross, within = call(
         ghosts_kernel,
-        [field, shape(4, levels, total, width), field, field, field, message, message],
+        [field, fields, field, field, field, edges, edges],
         aliases={2: 0, 3: 1, 4: 2, 5: 3},
         count=6,
     )(from_north, from_south, b_e, c_e, w_e, d_e)
-    cross, within = over_chips(cross), on_chip(within)
+    cross, within = exchanged(cross, within)
     scratch = (pltpu.VMEM((levels, total, width), F32),)
     q1, p1, w_next, cross, within, sums_1 = call(
         first_apply_kernel,
         [field, field, field, message, message, shape(3, 8, 128)],
-        count=9,
-        scratch=scratch,
-    )(b_e, c_e, w_e, d_e, p0, b_next, w_next_own, cross, within)
-    cross, within = over_chips(cross), on_chip(within)
+        count=10,
+        scratch=scratch * 3,
+    )(b_e, c_e, w_e, d_e, p0, cross_own, within_own, w_next_own, cross, within)
+    cross, within = exchanged(cross, within)
     q2, p2, cross, within, sums_2 = call(
         apply_kernel,
         [field, field, message, message, shape(2, 8, 128)],
         count=8,
         scratch=scratch,
     )(q1, c_e, w_e, d_e, p1, w_next, cross, within)
-    cross, within = over_chips(cross), on_chip(within)
+    cross, within = exchanged(cross, within)
     near, far = ("win_2", "tile"), ("win_0", "win_1")
     moments, q3 = call(
         moments_kernel, [shape(lax.axis_size(near), 8, 128), field], count=10, scratch=scratch
@@ -480,6 +538,4 @@
         P(WIN, "tile", None),
     )
     out_specs = (P(WIN, None, "tile", None), P(WIN, None, "tile", None))
-    return jax.shard_map(
-        on_device, mesh=split, in_specs=in_specs, out_specs=out_specs, check_vma=False
-    )
+    return jax.shard_map(solve, mesh=split, in_specs=in_specs, out_specs=out_specs, check_vma=False)

time: 105 us -> 95.3 us (0.908)
  waiting for transfers between devices: 21.2 us -> 9.24 us
  local copies, waits for them, and re-layouts: 5.21 us -> 0.01 us
  starting transfers between devices: 26.1 us -> 31 us
  blocking collectives: 43.7 us -> 46 us
    ppermute x4 -> x3, waiting for transfers between devices: 12.1 us -> 0.01 us  [shifted(): lax.ppermute(x, axis, [(i, i + by) for i in range(count) if 0 <= i + by <...]
    unnamed x12 -> x2, local copies, waits for them, and re-layouts: 5.21 us -> 0.01 us
    ppermute x3 -> x4, starting transfers between devices: 10.8 us -> 15.3 us  [over_chips(): return lax.ppermute(x, WIN, pairs + [(b, a) for a, b in pairs])]
    ppermute x3 -> x4, starting transfers between devices: 5.76 us -> 8.5 us  [on_chip(): return lax.ppermute(x, 'win_2', [(0, 1), (1, 0)])]
    ppermute x4 -> x3, starting transfers between devices: 9.57 us -> 7.17 us  [shifted(): lax.ppermute(x, axis, [(i, i + by) for i in range(count) if 0 <= i + by <...]
    all_to_all x2, blocking collectives: 43.7 us -> 46 us  [the longest x1 36.6 us: solve(): moments = lax.all_to_all(moments, far, 0, 0, tiled=True)]
    pallas_call x8 -> x7, Pallas kernels: 6.47 us -> 6.95 us  [the longest x1 2.68 us: solve(): call(pack_kernel, [ghost, ghost, field, fields, field, field, own, own],...]
    ppermute x3 -> x4, waiting for transfers between devices: 9.07 us -> 8.92 us  [over_chips(): return lax.ppermute(x, WIN, pairs + [(b, a) for a, b in pairs])]
  transfers between devices with their start and end apart: 10 -> 11, of which waited for: 6 -> 4; matrix products, arithmetic and copies ran while one was open for 0% -> 0% of each run, Pallas kernels for 0% -> 0%
where the time goes in v2:
time: 95.3 us; the launch traced here: 94 us
  blocking collectives  46 us (48%)
  starting transfers between devices  31 us (33%)
  waiting for transfers between devices  9.24 us (10%)
  Pallas kernels  6.95 us (7%)
    all_to_all x1, blocking collectives, solve(): moments = lax.all_to_all(moments, far, 0, 0, tiled=True)  36.6 us
    ppermute x4, starting transfers between devices, over_chips(): return lax.ppermute(x, WIN, pairs + [(b, a) for a, b in pairs])  15.3 us
    all_to_all x1, blocking collectives, solve(): moments = lax.all_to_all(moments, near, 0, 0, tiled=True)  9.45 us
    ppermute x4, waiting for transfers between devices, over_chips(): return lax.ppermute(x, WIN, pairs + [(b, a) for a, b in pairs])  8.92 us
    ppermute x4, starting transfers between devices, on_chip(): return lax.ppermute(x, 'win_2', [(0, 1), (1, 0)])  8.5 us
    ppermute x3, starting transfers between devices, shifted(): lax.ppermute(x, axis, [(i, i + by) for i in range(count) if 0 <= i + by <...  7.17 us
    pallas_call x1, Pallas kernels, solve(): call(pack_kernel, [ghost, ghost, field, fields, field, field, own, own],...  2.68 us
  transfers between devices with their start and end apart: 11, of which 4 were waited for; matrix products, arithmetic and copies ran while one was open for 0% of the time, Pallas kernels for 0%

profile of v2, /device:TPU:1, one launch (start us, length us, event | category | flops | bytes accessed | tf_op | source)
XLA Modules:
  0.0 94.0 jit_solution(9570599024514028851)
XLA Ops:
  0.6 0.0 copy-start
  0.6 2.7 %shard_map.77 = (f32[72,1024]{1,0:T(8,128)S(1)}, f32[72,1024]{1,0:T(8,128)S(1)}, f32[2,48,1024]{2,1,0:T(8,128)S(1)}, f32[4,2,48,1024]{3,2,1,0:T(8,128)S(1)}, f32...) custom-call(f32[2,32,1024]{2,1,0:T(8,128)} %bitcast.8, ...), custom_call_target="tpu_custom_call" | custom-call | tf_op jit(solution)/shard_map/pallas_call | solution.py:475
  3.3 4.0 %collective-permute-start = (f32[72,1024]{1,0:T(8,128)S(1)}, f32[72,1024]{1,0:T(8,128)S(1)}, u32[]{:S(2)}, u32[]{:S(2)}) collective-permute-start(f32[72,1024]{1,0:T(8,128)S(1)} %get-tuple-element.32), channel_id=1, source_target_pairs={{0,1},{1,2},{2,3},{4,5},{5,6},{6,7},{8,9},{9,10},{10,11},{12,13},{... | collective-permute-start | bytes 884744 | tf_op jit(solution)/shard_map/ppermute | solution.py:445
  7.3 1.3 %collective-permute-start.1 = (f32[72,1024]{1,0:T(8,128)S(1)}, f32[72,1024]{1,0:T(8,128)S(1)}, u32[]{:S(2)}, u32[]{:S(2)}) collective-permute-start(f32[72,1024]{1,0:T(8,128)S(1)} %get-tuple-element.33), channel_id=1, source_target_pairs={{1,0},{2,1},{3,2},{5,4},{6,5},{7,6},{9,8},{10,9},{11,10},{13,12},{... | collective-permute-start | bytes 884744 | tf_op jit(solution)/shard_map/ppermute | solution.py:445
  8.6 4.0 %collective-permute-start.2 = (f32[2,32,1024]{2,1,0:T(8,128)S(1)}, f32[2,32,1024]{2,1,0:T(8,128)S(1)}, u32[]{:S(2)}, u32[]{:S(2)}) collective-permute-start(f32[2,32,1024]{2,1,0:T(8,128)S(1)} %get-tuple-element.43), channel_id=1, source_target_pairs={{4,8},{12,16},{20,24},{28,32},{36,40},{44,48},{52,56},{60,64},{68,... | collective-permute-start | bytes 786440 | tf_op jit(solution)/shard_map/ppermute | solution.py:457
  12.6 2.7 %collective-permute-start.3 = (f32[2,32,1024]{2,1,0:T(8,128)S(1)}, f32[2,32,1024]{2,1,0:T(8,128)S(1)}, u32[]{:S(2)}, u32[]{:S(2)}) collective-permute-start(f32[2,32,1024]{2,1,0:T(8,128)S(1)} %get-tuple-element.44), channel_id=1, source_target_pairs={{0,4},{4,0},{1,5},{5,1},{2,6},{6,2},{3,7},{7,3},{8,12},{12,8},{9,1... | collective-permute-start | bytes 786440 | tf_op jit(solution)/shard_map/ppermute | solution.py:461
  15.4 0.0 copy-done
  15.4 1.9 %collective-permute-start.4 = (f32[2,32,1024]{2,1,0:T(8,128)S(1)}, f32[2,32,1024]{2,1,0:T(8,128)S(1)}, u32[]{:S(2)}, u32[]{:S(2)}) collective-permute-start(f32[2,32,1024]{2,1,0:T(8,128)S(1)} %bitcast.10), channel_id=1, source_target_pairs={{4,0},{8,4},{12,8},{16,12},{20,16},{24,20},{28,24},{32,28},{36,32}... | collective-permute-start | bytes 786440 | tf_op jit(solution)/shard_map/ppermute | solution.py:445
  17.3 0.0 collective-permute-done.from_north
  17.3 0.0 collective-permute-done.1.from_south
  17.3 0.4 shard_map.78
  17.8 4.3 %collective-permute-start.5 = (f32[40,1024]{1,0:T(8,128)S(1)}, f32[40,1024]{1,0:T(8,128)S(1)}, u32[]{:S(2)}, u32[]{:S(2)}) collective-permute-start(f32[40,1024]{1,0:T(8,128)S(1)} %get-tuple-element.45), channel_id=1, source_target_pairs={{4,8},{12,16},{20,24},{28,32},{36,40},{44,48},{52,56},{60,64},{68,... | collective-permute-start | bytes 491528 | tf_op jit(solution)/shard_map/ppermute | solution.py:457
  22.1 1.9 %collective-permute-start.6 = (f32[40,1024]{1,0:T(8,128)S(1)}, f32[40,1024]{1,0:T(8,128)S(1)}, u32[]{:S(2)}, u32[]{:S(2)}) collective-permute-start(f32[40,1024]{1,0:T(8,128)S(1)} %get-tuple-element.46), channel_id=1, source_target_pairs={{0,4},{4,0},{1,5},{5,1},{2,6},{6,2},{3,7},{7,3},{8,12},{12,8},{9,1... | collective-permute-start | bytes 491528 | tf_op jit(solution)/shard_map/ppermute | solution.py:461
  24.1 0.0 collective-permute-done.2.cross_own
  24.1 0.0 collective-permute-done.3.within_own
  24.1 0.0 collective-permute-done.4.w_next_own
  24.1 1.0 %collective-permute-done.5.cross_in = f32[40,1024]{1,0:T(8,128)S(1)} collective-permute-done((f32[40,1024]{1,0:T(8,128)S(1)}, f32[40,1024]{1,0:T(8,128)S(1)}, u32[]{:S(2)}, u32[]{:S(2)}) %collective-permute-start.5) | collective-permute-done | bytes 163872 | tf_op jit(solution)/shard_map/ppermute | solution.py:457
  25.1 0.3 collective-permute-done.6.within_in
  25.4 1.0 %shard_map.79 = (f32[2,48,1024]{2,1,0:T(8,128)S(1)}, f32[2,48,1024]{2,1,0:T(8,128)S(1)}, f32[2,48,1024]{2,1,0:T(8,128)S(1)}, f32[2,40,1024]{2,1,0:T(8,128)S(1)},...) custom-call(f32[2,48,1024]{2,1,0:T(8,128)S(1)} %get-tuple-element.38.b_e.q0, ...), custom_call_target="tpu_custom_call" | custom-call | tf_op jit(solution)/shard_map/pallas_call | solution.py:501
  26.4 3.4 %collective-permute-start.7 = (f32[2,40,1024]{2,1,0:T(8,128)S(1)}, f32[2,40,1024]{2,1,0:T(8,128)S(1)}, u32[]{:S(2)}, u32[]{:S(2)}) collective-permute-start(f32[2,40,1024]{2,1,0:T(8,128)S(1)} %get-tuple-element.50), channel_id=1, source_target_pairs={{4,8},{12,16},{20,24},{28,32},{36,40},{44,48},{52,56},{60,64},{68,... | collective-permute-start | bytes 983048 | tf_op jit(solution)/shard_map/ppermute | solution.py:457
  29.8 1.9 %collective-permute-start.8 = (f32[2,40,1024]{2,1,0:T(8,128)S(1)}, f32[2,40,1024]{2,1,0:T(8,128)S(1)}, u32[]{:S(2)}, u32[]{:S(2)}) collective-permute-start(f32[2,40,1024]{2,1,0:T(8,128)S(1)} %get-tuple-element.51), channel_id=1, source_target_pairs={{0,4},{4,0},{1,5},{5,1},{2,6},{6,2},{3,7},{7,3},{8,12},{12,8},{9,1... | collective-permute-start | bytes 983048 | tf_op jit(solution)/shard_map/ppermute | solution.py:461
  31.7 3.1 %collective-permute-done.7.cross_in = f32[2,40,1024]{2,1,0:T(8,128)S(1)} collective-permute-done((f32[2,40,1024]{2,1,0:T(8,128)S(1)}, f32[2,40,1024]{2,1,0:T(8,128)S(1)}, u32[]{:S(2)}, u32[]{:S(2)}) %collective-permute-start.7) | collective-permute-done | bytes 327712 | tf_op jit(solution)/shard_map/ppermute | solution.py:457
  34.8 0.0 collective-permute-done.8.within_in
  34.8 1.0 %shard_map.80 = (f32[2,48,1024]{2,1,0:T(8,128)S(1)}, f32[2,48,1024]{2,1,0:T(8,128)S(1)}, f32[2,40,1024]{2,1,0:T(8,128)S(1)}, f32[2,40,1024]{2,1,0:T(8,128)S(1)}, f32[2,8,128]{2,1,0:T(8,128)S(1)}) custom-call(f32[2,48,1024]{2,1,0:T(8,128)S(1)} %get-tuple-element.47.q1, f32[4,2,48,1024]{3,2,1,0:T(8,128)S(1)} %get-tuple-element.39.c, ...), custom_call_target="tpu_custom_call" | custom-call | tf_op jit(solution)/shard_map/pallas_call | solution.py:508
  35.8 1.9 %collective-permute-start.10 = (f32[2,40,1024]{2,1,0:T(8,128)S(1)}, f32[2,40,1024]{2,1,0:T(8,128)S(1)}, u32[]{:S(2)}, u32[]{:S(2)}) collective-permute-start(f32[2,40,1024]{2,1,0:T(8,128)S(1)} %get-tuple-element.55), channel_id=1, source_target_pairs={{0,4},{4,0},{1,5},{5,1},{2,6},{6,2},{3,7},{7,3},{8,12},{12,8},{9,1... | collective-permute-start | bytes 983048 | tf_op jit(solution)/shard_map/ppermute | solution.py:461
  37.7 3.6 %collective-permute-start.9 = (f32[2,40,1024]{2,1,0:T(8,128)S(1)}, f32[2,40,1024]{2,1,0:T(8,128)S(1)}, u32[]{:S(2)}, u32[]{:S(2)}) collective-permute-start(f32[2,40,1024]{2,1,0:T(8,128)S(1)} %get-tuple-element.54), channel_id=1, source_target_pairs={{4,8},{12,16},{20,24},{28,32},{36,40},{44,48},{52,56},{60,64},{68,... | collective-permute-start | bytes 983048 | tf_op jit(solution)/shard_map/ppermute | solution.py:457
  41.3 0.0 collective-permute-done.10.within_in
  41.3 4.8 %collective-permute-done.9.cross_in = f32[2,40,1024]{2,1,0:T(8,128)S(1)} collective-permute-done((f32[2,40,1024]{2,1,0:T(8,128)S(1)}, f32[2,40,1024]{2,1,0:T(8,128)S(1)}, u32[]{:S(2)}, u32[]{:S(2)}) %collective-permute-start.9) | collective-permute-done | bytes 327712 | tf_op jit(solution)/shard_map/ppermute | solution.py:457
  46.1 0.8 shard_map.81
  46.9 9.5 %all_to_all.10.x = f32[8,8,128]{2,1,0:T(8,128)S(1)} all-to-all(f32[8,8,128]{2,1,0:T(8,128)S(1)} %get-tuple-element.58), channel_id=1, replica_groups=mesh['win_0'=8,'win_1'=8,'win_2'=2,'tile'=4] {'win_2','tile'}, dimensions={0} | all-to-all | bytes 65536 | tf_op jit(solution)/shard_map/all_to_all | solution.py:519
  56.3 36.6 %all_to_all.11.parts = f32[64,8,128]{2,1,0:T(8,128)S(1)} all-to-all(f32[64,8,128]{2,1,0:T(8,128)S(1)} %shard_map.82), channel_id=1, replica_groups=mesh['win_0'=8,'win_1'=8,'win_2'=2,'tile'=4] {'win_0','win_1'}, dimensions={0} | all-to-all | bytes 524288 | tf_op jit(solution)/shard_map/all_to_all | solution.py:521
  92.9 1.1 %shard_map.83 = (f32[2,32,1024]{2,1,0:T(8,128)}, f32[2,32,1024]{2,1,0:T(8,128)}) custom-call(f32[64,8,128]{2,1,0:T(8,128)S(1)} %all_to_all.11.parts, f32[2,48,1024]{2,1,0:T(8,128)S(1)} %get-tuple-element.38.b_e.q0, f32[2,48,1024]{2,1,0:T(8,128)S(1)} %get-tuple-element.47.q1, f32[2,48,1024]{2,1,0:T(8,128)S(1)} %get-tuple-element.52.q2, ...), custom_call_target="tpu_custom_call" | custom-call | tf_op jit(solution)/shard_map/pallas_call | solution.py:522
  (1 shorter events, 0.0 us)
Async XLA Ops:
  0.6 14.8 %copy-start = (f32[1,2,32,1024]{3,2,1,0:T(8,128)S(1)}, f32[1,2,32,1024]{3,2,1,0:T(8,128)}, u32[]{:S(2)}) copy-start(f32[1,2,32,1024]{3,2,1,0:T(8,128)} %param.7) | copy-start | bytes 786436
  3.3 14.0 %collective-permute-start = (f32[72,1024]{1,0:T(8,128)S(1)}, f32[72,1024]{1,0:T(8,128)S(1)}, u32[]{:S(2)}, u32[]{:S(2)}) collective-permute-start(f32[72,1024]{1,0:T(8,128)S(1)} %get-tuple-element.32), channel_id=1, source_target_pairs={{0,1},{1,2},{2,3},{4,5},{5,6},{6,7},{8,9},{9,10},{10,11},{12,13},{... | collective-permute-start | bytes 884744 | tf_op jit(solution)/shard_map/ppermute | solution.py:445
  7.3 10.0 %collective-permute-start.1 = (f32[72,1024]{1,0:T(8,128)S(1)}, f32[72,1024]{1,0:T(8,128)S(1)}, u32[]{:S(2)}, u32[]{:S(2)}) collective-permute-start(f32[72,1024]{1,0:T(8,128)S(1)} %get-tuple-element.33), channel_id=1, source_target_pairs={{1,0},{2,1},{3,2},{5,4},{6,5},{7,6},{9,8},{10,9},{11,10},{13,12},{... | collective-permute-start | bytes 884744 | tf_op jit(solution)/shard_map/ppermute | solution.py:445
  8.6 15.5 %collective-permute-start.2 = (f32[2,32,1024]{2,1,0:T(8,128)S(1)}, f32[2,32,1024]{2,1,0:T(8,128)S(1)}, u32[]{:S(2)}, u32[]{:S(2)}) collective-permute-start(f32[2,32,1024]{2,1,0:T(8,128)S(1)} %get-tuple-element.43), channel_id=1, source_target_pairs={{4,8},{12,16},{20,24},{28,32},{36,40},{44,48},{52,56},{60,64},{68,... | collective-permute-start | bytes 786440 | tf_op jit(solution)/shard_map/ppermute | solution.py:457
  12.6 11.4 %collective-permute-start.3 = (f32[2,32,1024]{2,1,0:T(8,128)S(1)}, f32[2,32,1024]{2,1,0:T(8,128)S(1)}, u32[]{:S(2)}, u32[]{:S(2)}) collective-permute-start(f32[2,32,1024]{2,1,0:T(8,128)S(1)} %get-tuple-element.44), channel_id=1, source_target_pairs={{0,4},{4,0},{1,5},{5,1},{2,6},{6,2},{3,7},{7,3},{8,12},{12,8},{9,1... | collective-permute-start | bytes 786440 | tf_op jit(solution)/shard_map/ppermute | solution.py:461
  15.4 8.7 %collective-permute-start.4 = (f32[2,32,1024]{2,1,0:T(8,128)S(1)}, f32[2,32,1024]{2,1,0:T(8,128)S(1)}, u32[]{:S(2)}, u32[]{:S(2)}) collective-permute-start(f32[2,32,1024]{2,1,0:T(8,128)S(1)} %bitcast.10), channel_id=1, source_target_pairs={{4,0},{8,4},{12,8},{16,12},{20,16},{24,20},{28,24},{32,28},{36,32}... | collective-permute-start | bytes 786440 | tf_op jit(solution)/shard_map/ppermute | solution.py:445
  17.8 7.3 %collective-permute-start.5 = (f32[40,1024]{1,0:T(8,128)S(1)}, f32[40,1024]{1,0:T(8,128)S(1)}, u32[]{:S(2)}, u32[]{:S(2)}) collective-permute-start(f32[40,1024]{1,0:T(8,128)S(1)} %get-tuple-element.45), channel_id=1, source_target_pairs={{4,8},{12,16},{20,24},{28,32},{36,40},{44,48},{52,56},{60,64},{68,... | collective-permute-start | bytes 491528 | tf_op jit(solution)/shard_map/ppermute | solution.py:457
  22.1 3.3 %collective-permute-start.6 = (f32[40,1024]{1,0:T(8,128)S(1)}, f32[40,1024]{1,0:T(8,128)S(1)}, u32[]{:S(2)}, u32[]{:S(2)}) collective-permute-start(f32[40,1024]{1,0:T(8,128)S(1)} %get-tuple-element.46), channel_id=1, source_target_pairs={{0,4},{4,0},{1,5},{5,1},{2,6},{6,2},{3,7},{7,3},{8,12},{12,8},{9,1... | collective-permute-start | bytes 491528 | tf_op jit(solution)/shard_map/ppermute | solution.py:461
  26.4 8.4 %collective-permute-start.7 = (f32[2,40,1024]{2,1,0:T(8,128)S(1)}, f32[2,40,1024]{2,1,0:T(8,128)S(1)}, u32[]{:S(2)}, u32[]{:S(2)}) collective-permute-start(f32[2,40,1024]{2,1,0:T(8,128)S(1)} %get-tuple-element.50), channel_id=1, source_target_pairs={{4,8},{12,16},{20,24},{28,32},{36,40},{44,48},{52,56},{60,64},{68,... | collective-permute-start | bytes 983048 | tf_op jit(solution)/shard_map/ppermute | solution.py:457
  29.8 5.0 %collective-permute-start.8 = (f32[2,40,1024]{2,1,0:T(8,128)S(1)}, f32[2,40,1024]{2,1,0:T(8,128)S(1)}, u32[]{:S(2)}, u32[]{:S(2)}) collective-permute-start(f32[2,40,1024]{2,1,0:T(8,128)S(1)} %get-tuple-element.51), channel_id=1, source_target_pairs={{0,4},{4,0},{1,5},{5,1},{2,6},{6,2},{3,7},{7,3},{8,12},{12,8},{9,1... | collective-permute-start | bytes 983048 | tf_op jit(solution)/shard_map/ppermute | solution.py:461
  35.8 5.5 %collective-permute-start.10 = (f32[2,40,1024]{2,1,0:T(8,128)S(1)}, f32[2,40,1024]{2,1,0:T(8,128)S(1)}, u32[]{:S(2)}, u32[]{:S(2)}) collective-permute-start(f32[2,40,1024]{2,1,0:T(8,128)S(1)} %get-tuple-element.55), channel_id=1, source_target_pairs={{0,4},{4,0},{1,5},{5,1},{2,6},{6,2},{3,7},{7,3},{8,12},{12,8},{9,1... | collective-permute-start | bytes 983048 | tf_op jit(solution)/shard_map/ppermute | solution.py:461
  37.7 8.4 %collective-permute-start.9 = (f32[2,40,1024]{2,1,0:T(8,128)S(1)}, f32[2,40,1024]{2,1,0:T(8,128)S(1)}, u32[]{:S(2)}, u32[]{:S(2)}) collective-permute-start(f32[2,40,1024]{2,1,0:T(8,128)S(1)} %get-tuple-element.54), channel_id=1, source_target_pairs={{4,8},{12,16},{20,24},{28,32},{36,40},{44,48},{52,56},{60,64},{68,... | collective-permute-start | bytes 983048 | tf_op jit(solution)/shard_map/ppermute | solution.py:457

commit v3 on v2

--- a/solution.py
+++ b/solution.py
@@ -10,7 +10,6 @@
 WIN = ("win_0", "win_1", "win_2")
 THETA = 6.0
 G = 8
-HALO = 6
 F32 = jnp.float32
 
 
@@ -62,56 +61,43 @@
     return total
 
 
-PARTS = (("b", HALO), ("c", HALO - 1), ("w", HALO - 1), ("d", HALO - 2))
-PER_LEVEL = HALO + 5 * (HALO - 1) + (HALO - 2)
-
-
+PARTS = (("b", 0, 5), ("c", 0, 4), ("c", 1, 5), ("c", 2, 4), ("c", 3, 4), ("w", 0, 5), ("d", 0, 4), ("p", 0, 1))
+PER_LEVEL = sum(count for _, _, count in PARTS)
 EDGES = 20
-
-
-def message_rows(levels):
-    return -(-levels * PER_LEVEL // 8) * 8
 
 
 def ghost_items(levels):
     at = 0
     for lev in range(levels):
-        for name, rows in PARTS:
-            for f in range(4 if name == "c" else 1):
-                yield name, f, lev, at, rows
-                at += rows
+        for name, f, rows in PARTS:
+            yield name, f, lev, at, rows
+            at += rows
 
 
 def pack_kernel(
     b_hbm, c_hbm, w_hbm, pos_hbm, block_hbm, weight_hbm,
-    north, south, b_e, c_e, w_e, d_e, cross, within,
-    pos, block, weight, blocks, sems,
+    north, south, d_e,
+    pos, block, weight, blocks, b, c, w, sems,
 ):
     levels, rows, width = b_hbm.shape
     per_row = width // 128
-    own = pl.ds(G, rows)
-    moves = [
-        pltpu.make_async_copy(src, dst, sems.at[i])
-        for i, (src, dst) in enumerate(
-            (
-                (pos_hbm, pos),
-                (weight_hbm, weight),
-                (block_hbm, block),
-                (b_hbm, b_e.at[:, own, :]),
-                (c_hbm, c_e.at[:, :, own, :]),
-                (w_hbm, w_e.at[:, own, :]),
-            )
-        )
-    ]
+    pairs = [(pos_hbm, pos), (weight_hbm, weight), (block_hbm, block)]
+    for side, first in enumerate((0, rows - 8)):
+        edge = pl.ds(first, 8)
+        pairs += [
+            (b_hbm.at[:, edge, :], b.at[side]),
+            (c_hbm.at[:, :, edge, :], c.at[side]),
+            (w_hbm.at[:, edge, :], w.at[side]),
+        ]
+    moves = [pltpu.make_async_copy(src, dst, sems.at[i]) for i, (src, dst) in enumerate(pairs)]
     for move in moves:
         move.start()
     blank = jnp.zeros((G, width), F32)
     for lev in range(levels):
-        for out in (b_e.at[lev], w_e.at[lev], d_e.at[lev], *(c_e.at[f, lev] for f in range(4))):
-            out[0:G, :] = blank
-            out[G + rows :, :] = blank
+        d_e[lev, 0:G, :] = blank
+        d_e[lev, G + rows :, :] = blank
     blocks[...] = jnp.zeros(blocks.shape, F32)
-    for move in moves[:3]:
+    for move in moves:
         move.wait()
     pos_all, weight_all = pos[...], weight[...]
     n = pos_all.shape[0]
@@ -131,24 +117,38 @@
             d_e[lev, G : G + rows, j * 128 : j * 128 + 128] = blocks[
                 pl.ds(first, rows, stride=per_row), :
             ]
-    for move in moves[3:]:
-        move.wait()
     for name, f, lev, at, count in ghost_items(levels):
-        src = {"b": b_e, "w": w_e, "d": d_e}.get(name)
-        src = c_e.at[f] if src is None else src
-        north[at : at + count, :] = src[lev, G : G + count, :]
-        south[at : at + count, :] = src[lev, G + rows - count : G + rows, :]
-    used = levels * PER_LEVEL
-    for out in (north, south):
-        if out.shape[0] > used:
-            out[used:, :] = jnp.zeros((out.shape[0] - used, width), F32)
+        for side, out in enumerate((north, south)):
+            own = 0 if side == 0 else 8 - count
+            if name == "p":
+                image = model_tile(b.at[side], c.at[side], lev, 0, 1)
+                piece = image[4:5, :] if side == 0 else image[3:4, :]
+            elif name == "d":
+                own = G if side == 0 else G + rows - count
+                piece = d_e[lev, own : own + count, :]
+            elif name == "c":
+                piece = c[side, f, lev, own : own + count, :]
+            else:
+                piece = (b if name == "b" else w)[side, lev, own : own + count, :]
+            out[at : at + count, :] = piece
+
+
+def extend_kernel(b, c, w, b_e, c_e, w_e, cross, within):
+    levels, rows, width = b.shape
+    blank = jnp.zeros((G, width), F32)
+    for lev in range(levels):
+        targets = [(b_e.at[lev], b.at[lev]), (w_e.at[lev], w.at[lev])]
+        targets += [(c_e.at[f, lev], c.at[f, lev]) for f in range(4)]
+        for out, src in targets:
+            out[0:G, :] = blank
+            out[G : G + rows, :] = src[...]
+            out[G + rows :, :] = blank
 
     def send(forward, backward):
         for lev in range(levels):
-            backward[lev, :, :] = b_e[lev, G : G + rows, :]
-            for tile in range(1, 1 + rows // 8):
-                at = 8 * tile - G
-                forward[lev, at : at + 8, :] = model_tile(b_e, c_e, lev, tile, 2 + rows // 8)
+            backward[lev, :, :] = b[lev, :, :]
+            for tile in range(rows // 8):
+                forward[lev, 8 * tile : 8 * tile + 8, :] = model_tile(b, c, lev, tile, rows // 8)
 
     @pl.when(core_is_one())
     def _():
@@ -178,8 +178,9 @@
 
 
 def post(out, values, lev):
-    rows = out.shape[1]
-    out[lev, :, :] = values[lev, 4 : 4 + rows, :]
+    reach = out.shape[1] - (values.shape[1] - 2 * G)
+    first = G - reach // 2
+    out[lev, :, :] = values[lev, first : first + out.shape[1], :]
 
 
 def core_is_one():
@@ -189,12 +190,19 @@
 def ghosts_kernel(from_north, from_south, b_in, c_in, w_in, d_in, b_e, c_e, w_e, d_e, p, cross, within):
     levels, total, width = b_e.shape
     rows = total - 2 * G
-    for name, f, lev, at, count in ghost_items(levels):
-        out = {"b": b_e, "w": w_e, "d": d_e}.get(name)
-        out = c_e.at[f] if out is None else out
-        out[lev, G - count : G, :] = from_north[at : at + count, :]
-        out[lev, G + rows : G + rows + count, :] = from_south[at : at + count, :]
+
+    def fill(names):
+        for name, f, lev, at, count in ghost_items(levels):
+            if name in names:
+                out = {"b": b_e, "c": c_e.at[f], "w": w_e, "d": d_e, "p": p}[name]
+                reach = 5 if name == "p" else count
+                low, high = G - reach, G + rows + reach - count
+                out[lev, low : low + count, :] = from_north[at : at + count, :]
+                out[lev, high : high + count, :] = from_south[at : at + count, :]
+
+    fill("bcwd")
     propagate(b_e, c_e, p)
+    fill("p")
 
     def send(forward, backward):
         for lev in range(levels):
@@ -249,14 +257,16 @@
             out[lev, at, :] = value
 
 
-def products(pairs, levels, tiles, out):
-    for i, (x, y) in enumerate(pairs):
-        total = jnp.zeros((8, 128), F32)
-        for lev in range(levels):
-            for tile in range(1, tiles - 1):
-                at = slice(8 * tile, 8 * tile + 8)
-                total = total + folded(x[lev, at, :] * y[lev, at, :])
-        out[i] = total
+def products_kernel(x, y, out):
+    levels, total, _ = x.shape
+    totals = [jnp.zeros((8, 128), F32) for _ in range(out.shape[0])]
+    for lev in range(levels):
+        for at in range(G, total - G, 8):
+            u, v = x[lev, at : at + 8, :], y[lev, at : at + 8, :]
+            for i, (a, b) in enumerate(((u, v), (v, v), (u, u))[: len(totals)]):
+                totals[i] = totals[i] + folded(a * b)
+    for i, part in enumerate(totals):
+        out[i] = part
 
 
 def send_both(q, p, cross, within):
@@ -276,10 +286,9 @@
 
 def first_apply_kernel(
     b_e, c, w, d, p0, cross_own, within_own, w_next_own, cross_in, within_in,
-    q1, p1, w_next, cross, within, sums, edge, v_next, p_prev,
+    q1, p1, w_next, cross, within, edge, v_next, p_prev,
 ):
     levels, total, width = b_e.shape
-    tiles = total // 8
     rows = total - 2 * G
 
     def assemble(p_own, v_own, p_edges, v_edges):
@@ -316,13 +325,12 @@
     )
     propagate(q1, c, p1)
     send_both(q1, p1, cross, within)
-    products(((b_e, b_e), (b_e, q1), (q1, q1)), levels, tiles, sums)
 
 
 def apply_kernel(
-    q1, c, w, d, p1, w_next, cross_in, within_in, q2, p2, cross, within, sums, edge
+    q1, c, w, d, p1, w_next, cross_in, within_in, q2, p2, cross, within, edge
 ):
-    levels, total, _ = q1.shape
+    _, total, _ = q1.shape
     tiles = total // 8
     one = core_is_one()
 
@@ -342,10 +350,9 @@
     )
     propagate(q2, c, p2)
     send_both(q2, p2, cross, within)
-    products(((q1, q2), (q2, q2)), levels, tiles, sums)
-
-
-def moments_kernel(q2, c, w, d, p2, w_next, cross_in, within_in, sums_1, sums_2, out, q3, edge):
+
+
+def moments_kernel(q2, c, w, d, p2, w_next, cross_in, within_in, sums_1, sums_2, out, q3, edge, v_next, p_prev):
     levels, total, _ = q2.shape
     tiles = total // 8
     one = core_is_one()
@@ -353,43 +360,65 @@
         lax.axis_index("win_0") + lax.axis_index("win_1") == 0, jnp.logical_not(one)
     )
 
-    def v_next(lev, tile):
-        return jnp.where(
-            one, unposted(cross_in, lev, tile, tiles), unposted(within_in, lev, tile, tiles)
-        )
-
-    def p_prev(lev, tile):
-        return jnp.where(
-            one, unposted(within_in, lev, tile, tiles), unposted(cross_in, lev, tile, tiles)
-        )
+    @pl.when(one)
+    def _():
+        v_next[...] = cross_in[...]
+        p_prev[...] = within_in[...]
+
+    @pl.when(jnp.logical_not(one))
+    def _():
+        v_next[...] = within_in[...]
+        p_prev[...] = cross_in[...]
 
     last = jnp.zeros((8, 128), F32)
     for lev in range(levels):
         for tile in range(1, tiles - 1):
             at = slice(8 * tile, 8 * tile + 8)
-            here = q2[lev, at, :]
-            gap = v_next(lev, tile) - p2[lev, at, :]
-            own = d[lev, at, :] - THETA + jnp.where(first, w[lev, at, :], 0.0)
-            last = last + folded(w_next[lev, at, :] * gap * gap + own * here * here)
-    row = lax.broadcasted_iota(jnp.int32, (8, 128), 0)
-    result = jnp.zeros((8, 128), F32)
-    for i, part in enumerate([sums_1[0], sums_1[1], sums_1[2], sums_2[0], sums_2[1], last]):
-        total_i = jnp.sum(part, axis=0, keepdims=True)
-        result = jnp.where(row == i, jnp.broadcast_to(total_i, (8, 128)), result)
+            here, weight = q2[lev, at, :], w[lev, at, :]
+            gap = v_next[lev, 8 * tile - 4 : 8 * tile + 4, :] - p2[lev, at, :]
+            following = w_next[lev, at, :] * gap
+            diagonal = d[lev, at, :] - THETA
+            own = diagonal + jnp.where(first, weight, 0.0)
+            last = last + folded(following * gap + own * here * here)
+            edge[lev, at, :] = c[1, lev, at, :] * following
+            q3[lev, at, :] = (
+                (weight + diagonal) * here
+                - weight * p_prev[lev, 8 * tile - 4 : 8 * tile + 4, :]
+                - c[0, lev, at, :] * following
+                - west(c[2, lev, at, :] * following)
+                - east(c[3, lev, at, :] * following)
+            )
+        for row, at in ((G - 1, 3), (total - G, total - G - 4)):
+            following = w_next[lev, row : row + 1, :] * (
+                v_next[lev, at : at + 1, :] - p2[lev, row : row + 1, :]
+            )
+            edge[lev, row : row + 1, :] = c[1, lev, row : row + 1, :] * following
+        for tile in range(1, tiles - 1):
+            at = slice(8 * tile, 8 * tile + 8)
+            q3[lev, at, :] = q3[lev, at, :] - (
+                north_of(edge, lev, tile) + south_of(edge, lev, tile, tiles)
+            )
+    lane = lax.broadcasted_iota(jnp.int32, (1, 128), 1)
+    result = jnp.zeros((1, 128), F32)
+    parts = [sums_1[2], sums_1[0], sums_1[1], sums_2[0], sums_2[1], last]
+    for i, part in enumerate(parts):
+        total_i = jnp.sum(jnp.sum(part, axis=0, keepdims=True), axis=1, keepdims=True)
+        result = jnp.where(lane == i, jnp.broadcast_to(total_i, (1, 128)), result)
     for i in range(out.shape[0]):
         out[i] = result
-    second_half(
-        q2, c, w, d, p2, v_next,
-        lambda lev, tile: w_next[lev, 8 * tile : 8 * tile + 8, :], p_prev, q3, edge,
-    )
 
 
 def spread_kernel(x, out):
-    total = x[0]
-    for i in range(1, x.shape[0]):
-        total = total + x[i]
+    total = summed(x)
     for i in range(out.shape[0]):
         out[i] = total
+
+
+def summed(x):
+    parts = [x[i] for i in range(x.shape[0])]
+    while len(parts) > 1:
+        parts = [a + b for a, b in zip(parts[::2], parts[1::2])]
+    return parts[0]
 
 
 def times_a(v):
@@ -424,11 +453,8 @@
 
 def finish_kernel(parts, q0, q1, q2, q3, solution_field, residual):
     levels, rows, width = solution_field.shape
-    total = parts[0]
-    for i in range(1, parts.shape[0]):
-        total = total + parts[i]
-    summed = jnp.sum(total, axis=1, keepdims=True)
-    mu = [jnp.broadcast_to(summed[i : i + 1, :], (8, 128)) for i in range(6)]
+    total = summed(parts)
+    mu = [jnp.broadcast_to(total[:, i : i + 1], (8, 128)) for i in range(6)]
     x, r = coordinates(mu)
     wide = lambda v: jnp.concatenate([v] * (width // 128), axis=1)
     x = [wide(v) for v in x]
@@ -468,13 +494,14 @@
     field = shape(levels, total, width)
     fields = shape(4, levels, total, width)
     own = shape(levels, rows, width)
-    ghost = shape(message_rows(levels), width)
+    ghost = shape(levels * PER_LEVEL, width)
     edges = shape(levels * EDGES, width)
-    message = shape(levels, 40, width)
-
-    north, south, b_e, c_e, w_e, d_e, cross_own, within_own = call(
+    message = shape(levels, rows + 8, width)
+    scratch = pltpu.VMEM((levels, total, width), F32)
+
+    north, south, d_e = call(
         pack_kernel,
-        [ghost, ghost, field, fields, field, field, own, own],
+        [ghost, ghost, field],
         hbm=True,
         count=6,
         scratch=(
@@ -482,11 +509,17 @@
             pltpu.SMEM(obs_block.shape, jnp.int32),
             pltpu.VMEM(obs_weight.shape[1:], F32),
             pltpu.VMEM((b.size // 128, 128), F32),
-            pltpu.SemaphoreType.DMA((6,)),
+            pltpu.VMEM((2, levels, 8, width), F32),
+            pltpu.VMEM((2, 4, levels, 8, width), F32),
+            pltpu.VMEM((2, levels, 8, width), F32),
+            pltpu.SemaphoreType.DMA((9,)),
         ),
     )(*(in_hbm(x) for x in (b, c, w, obs_pos[0], obs_block, obs_weight[0])))
     from_south = shifted(north, "tile", -1)
     from_north = shifted(south, "tile", 1)
+    b_e, c_e, w_e, cross_own, within_own = call(
+        extend_kernel, [field, fields, field, own, own], count=3
+    )(b, c, w)
     cross_own = over_chips(cross_own)
     within_own = on_chip(within_own)
     w_next_own = shifted(w, WIN, -1)
@@ -497,31 +530,30 @@
         count=6,
     )(from_north, from_south, b_e, c_e, w_e, d_e)
     cross, within = exchanged(cross, within)
-    scratch = (pltpu.VMEM((levels, total, width), F32),)
-    q1, p1, w_next, cross, within, sums_1 = call(
+    q1, p1, w_next, cross, within = call(
         first_apply_kernel,
-        [field, field, field, message, message, shape(3, 8, 128)],
+        [field, field, field, message, message],
         count=10,
-        scratch=scratch * 3,
+        scratch=(scratch,) * 3,
     )(b_e, c_e, w_e, d_e, p0, cross_own, within_own, w_next_own, cross, within)
     cross, within = exchanged(cross, within)
-    q2, p2, cross, within, sums_2 = call(
-        apply_kernel,
-        [field, field, message, message, shape(2, 8, 128)],
-        count=8,
-        scratch=scratch,
+    (sums_1,) = call(products_kernel, [shape(3, 8, 128)], count=2)(b_e, q1)
+    q2, p2, cross, within = call(
+        apply_kernel, [field, field, message, message], count=8, scratch=(scratch,)
     )(q1, c_e, w_e, d_e, p1, w_next, cross, within)
     cross, within = exchanged(cross, within)
-    near, far = ("win_2", "tile"), ("win_0", "win_1")
+    (sums_2,) = call(products_kernel, [shape(2, 8, 128)], count=2)(q1, q2)
+    near, far = ("win_1", "tile"), ("win_0", "win_2")
     moments, q3 = call(
-        moments_kernel, [shape(lax.axis_size(near), 8, 128), field], count=10, scratch=scratch
+        moments_kernel,
+        [shape(lax.axis_size(near), 1, 128), field],
+        count=10,
+        scratch=(scratch,) + (pltpu.VMEM((levels, rows + 8, width), F32),) * 2,
     )(q2, c_e, w_e, d_e, p2, w_next, cross, within, sums_1, sums_2)
     moments = lax.all_to_all(moments, near, 0, 0, tiled=True)
-    (moments,) = call(spread_kernel, [shape(lax.axis_size(far), 8, 128)], count=1)(moments)
+    (moments,) = call(spread_kernel, [shape(lax.axis_size(far), 1, 128)], count=1)(moments)
     moments = lax.all_to_all(moments, far, 0, 0, tiled=True)
-    solution_field, residual = call(
-        finish_kernel, [shape(levels, rows, width), shape(levels, rows, width)], count=5
-    )(moments, b_e, q1, q2, q3)
+    solution_field, residual = call(finish_kernel, [own, own], count=5)(moments, b_e, q1, q2, q3)
     return solution_field[None], residual[None]
 
 

time: 95.3 us -> 93 us (0.976)
  starting transfers between devices: 31 us -> 29.9 us
    all_to_all x1, blocking collectives: 36.6 us -> 22.7 us  [solve(): moments = lax.all_to_all(moments, far, 0, 0, tiled=True)]
    all_to_all x1, blocking collectives: 9.45 us -> 22.4 us  [solve(): moments = lax.all_to_all(moments, near, 0, 0, tiled=True)]
    ppermute x4, starting transfers between devices: 15.3 us -> 14.2 us  [over_chips(): return lax.ppermute(x, WIN, pairs + [(b, a) for a, b in pairs])]
    pallas_call x6 -> x9, Pallas kernels: 6.51 us -> 6.66 us  [the longest x1 2.97 us: solve(): call(pack_kernel, [ghost, ghost, field], hbm=True, count=6, scratch=(pltp...]
  transfers between devices with their start and end apart: 11 -> 11, of which waited for: 4 -> 3; matrix products, arithmetic and copies ran while one was open for 0% -> 0% of each run, Pallas kernels for 0% -> 1%
where the time goes in v3:
time: 93 us; the launch traced here: 92.6 us
  blocking collectives  45.1 us (48%)
  starting transfers between devices  29.9 us (32%)
  waiting for transfers between devices  9.67 us (10%)
  Pallas kernels  7.05 us (8%)
    all_to_all x1, blocking collectives, solve(): moments = lax.all_to_all(moments, far, 0, 0, tiled=True)  22.7 us
    all_to_all x1, blocking collectives, solve(): moments = lax.all_to_all(moments, near, 0, 0, tiled=True)  22.4 us
    ppermute x4, starting transfers between devices, over_chips(): return lax.ppermute(x, WIN, pairs + [(b, a) for a, b in pairs])  14.2 us
    ppermute x4, waiting for transfers between devices, over_chips(): return lax.ppermute(x, WIN, pairs + [(b, a) for a, b in pairs])  9.65 us
    ppermute x4, starting transfers between devices, on_chip(): return lax.ppermute(x, 'win_2', [(0, 1), (1, 0)])  8.5 us
    ppermute x3, starting transfers between devices, shifted(): lax.ppermute(x, axis, [(i, i + by) for i in range(count) if 0 <= i + by <...  7.16 us
    pallas_call x1, Pallas kernels, solve(): call(pack_kernel, [ghost, ghost, field], hbm=True, count=6, scratch=(pltp...  2.97 us
  transfers between devices with their start and end apart: 11, of which 3 were waited for; matrix products, arithmetic and copies ran while one was open for 0% of the time, Pallas kernels for 1%

profile of v3, /device:TPU:1, one launch (start us, length us, event | category | flops | bytes accessed | tf_op | source)
XLA Modules:
  0.0 92.6 jit_solution(18054438202867665668)
XLA Ops:
  0.7 3.0 %shard_map.77 = (f32[64,1024]{1,0:T(8,128)S(1)}, f32[64,1024]{1,0:T(8,128)S(1)}, f32[2,48,1024]{2,1,0:T(8,128)S(1)}) custom-call(f32[2,32,1024]{2,1,0:T(8,128)} %bitcast.9, f32[4,2,32,1024]{3,2,1,0:T(8,128)} %bitcast.7, f32[2,32,1024]{2,1,0:T(8,128)} %bitcast.11, s32[32,128]{1,0:T(8,128)} %bitcast.14, s32[1,32]{1,0:T(1,128)} %block_hbm.1, f32[32,128]{1,0:T(8,128)} %bitcast.15), custom_call_target="tpu_custom_call" | custom-call | tf_op jit(solution)/shard_map/pallas_call | solution.py:502
  3.6 3.9 %collective-permute-start = (f32[64,1024]{1,0:T(8,128)S(1)}, f32[64,1024]{1,0:T(8,128)S(1)}, u32[]{:S(2)}, u32[]{:S(2)}) collective-permute-start(f32[64,1024]{1,0:T(8,128)S(1)} %get-tuple-element.30), channel_id=1, source_target_pairs={{0,1},{1,2},{2,3},{4,5},{5,6},{6,7},{8,9},{9,10},{10,11},{12,13},{... | collective-permute-start | bytes 786440 | tf_op jit(solution)/shard_map/ppermute | solution.py:471
  7.6 1.3 %collective-permute-start.1 = (f32[64,1024]{1,0:T(8,128)S(1)}, f32[64,1024]{1,0:T(8,128)S(1)}, u32[]{:S(2)}, u32[]{:S(2)}) collective-permute-start(f32[64,1024]{1,0:T(8,128)S(1)} %get-tuple-element.31), channel_id=1, source_target_pairs={{1,0},{2,1},{3,2},{5,4},{6,5},{7,6},{9,8},{10,9},{11,10},{13,12},{... | collective-permute-start | bytes 786440 | tf_op jit(solution)/shard_map/ppermute | solution.py:471
  8.9 0.4 shard_map.78
  9.3 4.0 %collective-permute-start.2 = (f32[2,32,1024]{2,1,0:T(8,128)S(1)}, f32[2,32,1024]{2,1,0:T(8,128)S(1)}, u32[]{:S(2)}, u32[]{:S(2)}) collective-permute-start(f32[2,32,1024]{2,1,0:T(8,128)S(1)} %get-tuple-element.41), channel_id=1, source_target_pairs={{4,8},{12,16},{20,24},{28,32},{36,40},{44,48},{52,56},{60,64},{68,... | collective-permute-start | bytes 786440 | tf_op jit(solution)/shard_map/ppermute | solution.py:483
  13.3 2.7 %collective-permute-start.3 = (f32[2,32,1024]{2,1,0:T(8,128)S(1)}, f32[2,32,1024]{2,1,0:T(8,128)S(1)}, u32[]{:S(2)}, u32[]{:S(2)}) collective-permute-start(f32[2,32,1024]{2,1,0:T(8,128)S(1)} %get-tuple-element.42), channel_id=1, source_target_pairs={{0,4},{4,0},{1,5},{5,1},{2,6},{6,2},{3,7},{7,3},{8,12},{12,8},{9,1... | collective-permute-start | bytes 786440 | tf_op jit(solution)/shard_map/ppermute | solution.py:487
  16.1 1.9 %collective-permute-start.4 = (f32[2,32,1024]{2,1,0:T(8,128)S(1)}, f32[2,32,1024]{2,1,0:T(8,128)S(1)}, u32[]{:S(2)}, u32[]{:S(2)}) collective-permute-start(f32[2,32,1024]{2,1,0:T(8,128)S(1)} %bitcast.13), channel_id=1, source_target_pairs={{4,0},{8,4},{12,8},{16,12},{20,16},{24,20},{28,24},{32,28},{36,32}... | collective-permute-start | bytes 786440 | tf_op jit(solution)/shard_map/ppermute | solution.py:471
  18.0 0.0 collective-permute-done.from_north
  18.0 0.0 collective-permute-done.1.from_south
  18.0 0.4 shard_map.79
  18.4 3.6 %collective-permute-start.5 = (f32[40,1024]{1,0:T(8,128)S(1)}, f32[40,1024]{1,0:T(8,128)S(1)}, u32[]{:S(2)}, u32[]{:S(2)}) collective-permute-start(f32[40,1024]{1,0:T(8,128)S(1)} %get-tuple-element.43), channel_id=1, source_target_pairs={{4,8},{12,16},{20,24},{28,32},{36,40},{44,48},{52,56},{60,64},{68,... | collective-permute-start | bytes 491528 | tf_op jit(solution)/shard_map/ppermute | solution.py:483
  22.1 1.9 %collective-permute-start.6 = (f32[40,1024]{1,0:T(8,128)S(1)}, f32[40,1024]{1,0:T(8,128)S(1)}, u32[]{:S(2)}, u32[]{:S(2)}) collective-permute-start(f32[40,1024]{1,0:T(8,128)S(1)} %get-tuple-element.44), channel_id=1, source_target_pairs={{0,4},{4,0},{1,5},{5,1},{2,6},{6,2},{3,7},{7,3},{8,12},{12,8},{9,1... | collective-permute-start | bytes 491528 | tf_op jit(solution)/shard_map/ppermute | solution.py:487
  24.0 0.0 collective-permute-done.2.cross_own
  24.0 0.0 collective-permute-done.3.within_own
  24.0 0.0 collective-permute-done.4.w_next_own
  24.1 1.5 %collective-permute-done.5.cross_in = f32[40,1024]{1,0:T(8,128)S(1)} collective-permute-done((f32[40,1024]{1,0:T(8,128)S(1)}, f32[40,1024]{1,0:T(8,128)S(1)}, u32[]{:S(2)}, u32[]{:S(2)}) %collective-permute-start.5) | collective-permute-done | bytes 163872 | tf_op jit(solution)/shard_map/ppermute | solution.py:483
  25.5 0.9 shard_map.80
  26.4 3.2 %collective-permute-start.7 = (f32[2,40,1024]{2,1,0:T(8,128)S(1)}, f32[2,40,1024]{2,1,0:T(8,128)S(1)}, u32[]{:S(2)}, u32[]{:S(2)}) collective-permute-start(f32[2,40,1024]{2,1,0:T(8,128)S(1)} %get-tuple-element.48), channel_id=1, source_target_pairs={{4,8},{12,16},{20,24},{28,32},{36,40},{44,48},{52,56},{60,64},{68,... | collective-permute-start | bytes 983048 | tf_op jit(solution)/shard_map/ppermute | solution.py:483
  29.6 1.9 %collective-permute-start.8 = (f32[2,40,1024]{2,1,0:T(8,128)S(1)}, f32[2,40,1024]{2,1,0:T(8,128)S(1)}, u32[]{:S(2)}, u32[]{:S(2)}) collective-permute-start(f32[2,40,1024]{2,1,0:T(8,128)S(1)} %get-tuple-element.49), channel_id=1, source_target_pairs={{0,4},{4,0},{1,5},{5,1},{2,6},{6,2},{3,7},{7,3},{8,12},{12,8},{9,1... | collective-permute-start | bytes 983048 | tf_op jit(solution)/shard_map/ppermute | solution.py:487
  31.5 3.3 %collective-permute-done.7.cross_in = f32[2,40,1024]{2,1,0:T(8,128)S(1)} collective-permute-done((f32[2,40,1024]{2,1,0:T(8,128)S(1)}, f32[2,40,1024]{2,1,0:T(8,128)S(1)}, u32[]{:S(2)}, u32[]{:S(2)}) %collective-permute-start.7) | collective-permute-done | bytes 327712 | tf_op jit(solution)/shard_map/ppermute | solution.py:483
  34.8 0.0 collective-permute-done.8.within_in
  34.8 0.8 shard_map.81
  35.6 1.9 %collective-permute-start.10 = (f32[2,40,1024]{2,1,0:T(8,128)S(1)}, f32[2,40,1024]{2,1,0:T(8,128)S(1)}, u32[]{:S(2)}, u32[]{:S(2)}) collective-permute-start(f32[2,40,1024]{2,1,0:T(8,128)S(1)} %get-tuple-element.53), channel_id=1, source_target_pairs={{0,4},{4,0},{1,5},{5,1},{2,6},{6,2},{3,7},{7,3},{8,12},{12,8},{9,1... | collective-permute-start | bytes 983048 | tf_op jit(solution)/shard_map/ppermute | solution.py:487
  37.6 3.4 %collective-permute-start.9 = (f32[2,40,1024]{2,1,0:T(8,128)S(1)}, f32[2,40,1024]{2,1,0:T(8,128)S(1)}, u32[]{:S(2)}, u32[]{:S(2)}) collective-permute-start(f32[2,40,1024]{2,1,0:T(8,128)S(1)} %get-tuple-element.52), channel_id=1, source_target_pairs={{4,8},{12,16},{20,24},{28,32},{36,40},{44,48},{52,56},{60,64},{68,... | collective-permute-start | bytes 983048 | tf_op jit(solution)/shard_map/ppermute | solution.py:483
  40.9 0.1 shard_map.82.sums_1
  41.0 0.1 shard_map.83.sums_2
  41.1 0.0 collective-permute-done.10.within_in
  41.1 4.9 %collective-permute-done.9.cross_in = f32[2,40,1024]{2,1,0:T(8,128)S(1)} collective-permute-done((f32[2,40,1024]{2,1,0:T(8,128)S(1)}, f32[2,40,1024]{2,1,0:T(8,128)S(1)}, u32[]{:S(2)}, u32[]{:S(2)}) %collective-permute-start.9) | collective-permute-done | bytes 327712 | tf_op jit(solution)/shard_map/ppermute | solution.py:483
  46.0 0.4 shard_map.84
  46.4 22.4 %all_to_all.10.x = f32[32,1,128]{2,1,0:T(1,128)S(1)} all-to-all(f32[32,1,128]{2,1,0:T(1,128)S(1)} %get-tuple-element.54), channel_id=1, replica_groups=mesh['win_0'=8,'win_1'=8,'win_2'=2,'tile'=4] {'win_1','tile'}, dimensions={0} | all-to-all | bytes 32768 | tf_op jit(solution)/shard_map/all_to_all | solution.py:553
  68.8 22.7 %all_to_all.11.parts = f32[16,1,128]{2,1,0:T(1,128)S(1)} all-to-all(f32[16,1,128]{2,1,0:T(1,128)S(1)} %shard_map.85), channel_id=1, replica_groups=mesh['win_0'=8,'win_1'=8,'win_2'=2,'tile'=4] {'win_0','win_2'}, dimensions={0} | all-to-all | bytes 16384 | tf_op jit(solution)/shard_map/all_to_all | solution.py:555
  91.5 1.1 %shard_map.86 = (f32[2,32,1024]{2,1,0:T(8,128)}, f32[2,32,1024]{2,1,0:T(8,128)}) custom-call(f32[16,1,128]{2,1,0:T(1,128)S(1)} %all_to_all.11.parts, f32[2,48,1024]{2,1,0:T(8,128)S(1)} %get-tuple-element.36.b_e.x.q0, f32[2,48,1024]{2,1,0:T(8,128)S(1)} %get-tuple-element.45.q1.y.x, f32[2,48,1024]{2,1,0:T(8,128)S(1)} %get-tuple-element.50.y.q2, ...), custom_call_target="tpu_custom_call" | custom-call | tf_op jit(solution)/shard_map/pallas_call | solution.py:556
  (8 shorter events, 0.0 us)
Async XLA Ops:
  0.6 8.3 %copy-start.2 = (f32[1,2,32,1024]{3,2,1,0:T(8,128)S(1)}, f32[1,2,32,1024]{3,2,1,0:T(8,128)}, u32[]{:S(2)}) copy-start(f32[1,2,32,1024]{3,2,1,0:T(8,128)} %param.7) | copy-start | bytes 786436
  0.6 8.3 %copy-start.1 = (f32[1,2,32,1024]{3,2,1,0:T(8,128)S(1)}, f32[1,2,32,1024]{3,2,1,0:T(8,128)}, u32[]{:S(2)}) copy-start(f32[1,2,32,1024]{3,2,1,0:T(8,128)} %param.6) | copy-start | bytes 786436
  0.7 8.3 %copy-start = (f32[4,1,2,32,1024]{4,3,2,1,0:T(8,128)S(1)}, f32[4,1,2,32,1024]{4,3,2,1,0:T(8,128)}, u32[]{:S(2)}) copy-start(f32[4,1,2,32,1024]{4,3,2,1,0:T(8,128)} %param.8) | copy-start | bytes 3145732
  3.6 14.4 %collective-permute-start = (f32[64,1024]{1,0:T(8,128)S(1)}, f32[64,1024]{1,0:T(8,128)S(1)}, u32[]{:S(2)}, u32[]{:S(2)}) collective-permute-start(f32[64,1024]{1,0:T(8,128)S(1)} %get-tuple-element.30), channel_id=1, source_target_pairs={{0,1},{1,2},{2,3},{4,5},{5,6},{6,7},{8,9},{9,10},{10,11},{12,13},{... | collective-permute-start | bytes 786440 | tf_op jit(solution)/shard_map/ppermute | solution.py:471
  7.6 10.4 %collective-permute-start.1 = (f32[64,1024]{1,0:T(8,128)S(1)}, f32[64,1024]{1,0:T(8,128)S(1)}, u32[]{:S(2)}, u32[]{:S(2)}) collective-permute-start(f32[64,1024]{1,0:T(8,128)S(1)} %get-tuple-element.31), channel_id=1, source_target_pairs={{1,0},{2,1},{3,2},{5,4},{6,5},{7,6},{9,8},{10,9},{11,10},{13,12},{... | collective-permute-start | bytes 786440 | tf_op jit(solution)/shard_map/ppermute | solution.py:471
  9.3 14.7 %collective-permute-start.2 = (f32[2,32,1024]{2,1,0:T(8,128)S(1)}, f32[2,32,1024]{2,1,0:T(8,128)S(1)}, u32[]{:S(2)}, u32[]{:S(2)}) collective-permute-start(f32[2,32,1024]{2,1,0:T(8,128)S(1)} %get-tuple-element.41), channel_id=1, source_target_pairs={{4,8},{12,16},{20,24},{28,32},{36,40},{44,48},{52,56},{60,64},{68,... | collective-permute-start | bytes 786440 | tf_op jit(solution)/shard_map/ppermute | solution.py:483
  13.3 10.7 %collective-permute-start.3 = (f32[2,32,1024]{2,1,0:T(8,128)S(1)}, f32[2,32,1024]{2,1,0:T(8,128)S(1)}, u32[]{:S(2)}, u32[]{:S(2)}) collective-permute-start(f32[2,32,1024]{2,1,0:T(8,128)S(1)} %get-tuple-element.42), channel_id=1, source_target_pairs={{0,4},{4,0},{1,5},{5,1},{2,6},{6,2},{3,7},{7,3},{8,12},{12,8},{9,1... | collective-permute-start | bytes 786440 | tf_op jit(solution)/shard_map/ppermute | solution.py:487
  16.1 7.9 %collective-permute-start.4 = (f32[2,32,1024]{2,1,0:T(8,128)S(1)}, f32[2,32,1024]{2,1,0:T(8,128)S(1)}, u32[]{:S(2)}, u32[]{:S(2)}) collective-permute-start(f32[2,32,1024]{2,1,0:T(8,128)S(1)} %bitcast.13), channel_id=1, source_target_pairs={{4,0},{8,4},{12,8},{16,12},{20,16},{24,20},{28,24},{32,28},{36,32}... | collective-permute-start | bytes 786440 | tf_op jit(solution)/shard_map/ppermute | solution.py:471
  18.4 7.1 %collective-permute-start.5 = (f32[40,1024]{1,0:T(8,128)S(1)}, f32[40,1024]{1,0:T(8,128)S(1)}, u32[]{:S(2)}, u32[]{:S(2)}) collective-permute-start(f32[40,1024]{1,0:T(8,128)S(1)} %get-tuple-element.43), channel_id=1, source_target_pairs={{4,8},{12,16},{20,24},{28,32},{36,40},{44,48},{52,56},{60,64},{68,... | collective-permute-start | bytes 491528 | tf_op jit(solution)/shard_map/ppermute | solution.py:483
  22.1 3.5 %collective-permute-start.6 = (f32[40,1024]{1,0:T(8,128)S(1)}, f32[40,1024]{1,0:T(8,128)S(1)}, u32[]{:S(2)}, u32[]{:S(2)}) collective-permute-start(f32[40,1024]{1,0:T(8,128)S(1)} %get-tuple-element.44), channel_id=1, source_target_pairs={{0,4},{4,0},{1,5},{5,1},{2,6},{6,2},{3,7},{7,3},{8,12},{12,8},{9,1... | collective-permute-start | bytes 491528 | tf_op jit(solution)/shard_map/ppermute | solution.py:487
  26.4 8.4 %collective-permute-start.7 = (f32[2,40,1024]{2,1,0:T(8,128)S(1)}, f32[2,40,1024]{2,1,0:T(8,128)S(1)}, u32[]{:S(2)}, u32[]{:S(2)}) collective-permute-start(f32[2,40,1024]{2,1,0:T(8,128)S(1)} %get-tuple-element.48), channel_id=1, source_target_pairs={{4,8},{12,16},{20,24},{28,32},{36,40},{44,48},{52,56},{60,64},{68,... | collective-permute-start | bytes 983048 | tf_op jit(solution)/shard_map/ppermute | solution.py:483
  29.6 5.2 %collective-permute-start.8 = (f32[2,40,1024]{2,1,0:T(8,128)S(1)}, f32[2,40,1024]{2,1,0:T(8,128)S(1)}, u32[]{:S(2)}, u32[]{:S(2)}) collective-permute-start(f32[2,40,1024]{2,1,0:T(8,128)S(1)} %get-tuple-element.49), channel_id=1, source_target_pairs={{0,4},{4,0},{1,5},{5,1},{2,6},{6,2},{3,7},{7,3},{8,12},{12,8},{9,1... | collective-permute-start | bytes 983048 | tf_op jit(solution)/shard_map/ppermute | solution.py:487
  35.6 5.4 %collective-permute-start.10 = (f32[2,40,1024]{2,1,0:T(8,128)S(1)}, f32[2,40,1024]{2,1,0:T(8,128)S(1)}, u32[]{:S(2)}, u32[]{:S(2)}) collective-permute-start(f32[2,40,1024]{2,1,0:T(8,128)S(1)} %get-tuple-element.53), channel_id=1, source_target_pairs={{0,4},{4,0},{1,5},{5,1},{2,6},{6,2},{3,7},{7,3},{8,12},{12,8},{9,1... | collective-permute-start | bytes 983048 | tf_op jit(solution)/shard_map/ppermute | solution.py:487
  37.6 8.4 %collective-permute-start.9 = (f32[2,40,1024]{2,1,0:T(8,128)S(1)}, f32[2,40,1024]{2,1,0:T(8,128)S(1)}, u32[]{:S(2)}, u32[]{:S(2)}) collective-permute-start(f32[2,40,1024]{2,1,0:T(8,128)S(1)} %get-tuple-element.52), channel_id=1, source_target_pairs={{4,8},{12,16},{20,24},{28,32},{36,40},{44,48},{52,56},{60,64},{68,... | collective-permute-start | bytes 983048 | tf_op jit(solution)/shard_map/ppermute | solution.py:483
